TPU v7x, 32 devices: a whole 2x2x4 slice. The times are simulated.
32 devices in a mesh: req: 2 (over y), patch: 16 (over z, x, core).
Axes of the slice: x: 2, y: 2, z: 4, core: 2. Of those that a mesh axis runs over, the one named last changes fastest.
Arguments:
- tokens: bfloat16 [1536, 1152], P(('req', 'patch')), parts along dimension 0, may hold values from -6 to 6
- positions: int32 [2, 1536], P(None, ('req', 'patch')), parts along dimension 1, may hold values from 0 to 95
- counts: int32 [32], P('req'), parts along dimension 0, may hold values from 1 to 48, 384 in all
- timestep: int32 [2], P('req'), parts along dimension 0, may hold values from 0 to 999
- time_in: bfloat16 [256, 1152], replicated, may hold values from -0.375 to 0.375
- time_out: bfloat16 [1152, 1152], P(None, 'patch'), may hold values from -0.1875 to 0.1875
- ada_weight: bfloat16 [1152, 3456], P('patch'), may hold values from -0.375 to 0.375
- qkv_weight: bfloat16 [1152, 3456], replicated, may hold values from -2 to 2, as said below
- out_weight: bfloat16 [1152, 1152], replicated, may hold values from -0.1875 to 0.1875
Outputs:
- block_out: bfloat16 [1536, 1152], P(('req', 'patch')), parts along dimension 0
There are 2 independent parts, one for each index of `req`. A program takes and returns all parts, laid end to end along the dimension named above; an argument that names none is the same for every part. Nothing has to cross between parts.
Inputs may be any that keep to these rules, and one draw needn't show every extreme that they name: `counts`: used slots are the first ones of each block; they sum to exactly 384, and some block uses all 48. `qkv_weight`: columns are 1152 of queries, 1152 of keys, 1152 of values, each head's 72 columns side by side.
All inputs are finite; a program needn't handle non-finite values.
Results may differ from a plain program's by a relative error of at most 0.0039.
Values may be sent and summed in bfloat16 or wider, within the bound.
A program may use at most 64 MiB of HBM per device.

v0:
```python
import functools
import math

import jax
import jax.numpy as jnp
import numpy as np
from jax import lax
from jax.experimental import pallas as pl
from jax.experimental.pallas import tpu as pltpu
from jax.sharding import PartitionSpec as P

HEADS = 16
NEG = -1e30
F32 = jnp.float32
BF16 = jnp.bfloat16
MESH = pl.DeviceIdType.MESH


def silu(v):
    return v / (1.0 + jnp.exp(-v))


def dot(a, b):
    return jnp.dot(a, b, preferred_element_type=F32)


def one_row_dot(row, matrix):
    wide = jnp.broadcast_to(row, (16, row.shape[1])).astype(BF16)
    return dot(wide, matrix)[0:1]


def fold_group(rows, extra):
    group = 8
    while rows // group * extra > 128:
        group *= 2
    return group


def fold(block):
    rows, extra = block.shape[0], block.shape[1] - 64
    group = fold_group(rows, extra)
    half = rows // 2
    main = jnp.concatenate([block[:half, :64], block[half:, :64]], axis=1)
    pieces = [block[r : r + group, 64:] for r in range(0, rows, group)]
    spare = 128 - extra * len(pieces)
    rest = jnp.concatenate(pieces + [jnp.zeros((group, spare), F32)], axis=1)
    return jnp.concatenate([main, rest], axis=0)


def unfold(packed, rows, extra):
    half = rows // 2
    left = jnp.concatenate([packed[:half, :64], packed[:half, 64:]], axis=0)
    rest = packed[half:]
    count = rows // fold_group(rows, extra)
    right = jnp.concatenate([rest[:, r * extra : (r + 1) * extra] for r in range(count)], axis=0)
    return jnp.concatenate([left, right], axis=1)


def block_kernel(
    n, rows, width, head,
    counts, tstep, pos, pos_tab, time_tab,
    tok_h, tin_h, tout_h, ada_h, qkv_h, ow_h,
    out,
    tok, tin, tout, ada, qkv, ow, mods, gates, xin_s, norm_s, send, got, kbuf, vbuf, att, back,
    done, osem, lsem, wsem, msend, mrecv, gsend, grecv, psend, precv, asend, arecv,
):
    me = lax.axis_index("patch")
    my_head = lax.rem(me, HEADS)
    group = me // HEADS
    chunk = HEADS * rows
    groups = n // HEADS
    inv_root = math.log2(math.e) / math.sqrt(head)

    barrier = pltpu.get_barrier_semaphore()

    @pl.loop(1, n)
    def _(step):
        pl.semaphore_signal(
            barrier, inc=1, device_id={"patch": lax.rem(me + step, n)}, device_id_type=MESH
        )

    loads = [
        pltpu.make_async_copy(src, dst, lsem.at[i])
        for i, (src, dst) in enumerate(
            [(tin_h, tin), (tout_h, tout), (ada_h, ada), (tok_h, tok), (qkv_h, qkv)]
        )
    ]
    for load in loads[:3]:
        load.start()

    angles = tstep[0].astype(F32) * time_tab[0:1, :] + time_tab[1:2, :]
    features = jnp.sin(angles).astype(BF16)
    loads[0].wait()
    hidden = silu(one_row_dot(features, tin[...])).astype(BF16)
    loads[1].wait()
    wide = jnp.broadcast_to(hidden, (16, width))
    cond = lax.dot_general(wide, tout[...], (((1,), (1,)), ((), ())), preferred_element_type=F32)
    activated = silu(cond[0:1]).astype(BF16)
    loads[2].wait()
    partial = one_row_dot(activated, ada[...])
    mods[me] = jnp.concatenate(
        [partial[:, :width], partial[:, width : 2 * width]], axis=0
    ).astype(BF16)
    span = gates.shape[2]
    gates[me] = jnp.concatenate(
        [partial[:, 2 * width : 2 * width + span], partial[:, 3 * width - span :]], axis=0
    ).astype(BF16)
    for load in loads[3:]:
        load.start()

    pl.semaphore_wait(barrier, n - 1)

    def mod_copy(step, slot):
        return pltpu.make_async_remote_copy(
            src_ref=mods.at[slot],
            dst_ref=mods.at[slot],
            send_sem=msend.at[step],
            recv_sem=mrecv.at[slot],
            device_id={"patch": lax.rem(me + step, n)},
            device_id_type=MESH,
        )

    def gate_copy(step, slot):
        return pltpu.make_async_remote_copy(
            src_ref=gates.at[slot],
            dst_ref=gates.at[slot],
            send_sem=gsend.at[step],
            recv_sem=grecv.at[slot],
            device_id={"patch": lax.rem(me + step, n)},
            device_id_type=MESH,
        )

    @pl.loop(1, n)
    def _(step):
        mod_copy(step, me).start()

    ow[:, head:, :] = jnp.zeros((HEADS, ow.shape[1] - head, width), BF16)
    ow_loads = [
        pltpu.make_async_copy(
            ow_h.at[pl.ds(h * head, head), :], ow.at[h, pl.ds(0, head), :], wsem.at[h]
        )
        for h in range(HEADS)
    ]
    for load in ow_loads:
        load.start()

    ids = lax.broadcasted_iota(jnp.int32, (rows, rows), 0)
    eye = ids == lax.broadcasted_iota(jnp.int32, (rows, rows), 1)
    posf = pos[...].astype(F32)
    row_col = jnp.sum(jnp.where(eye, posf[0:1, :], 0.0), axis=1, keepdims=True)
    col_col = jnp.sum(jnp.where(eye, posf[1:2, :], 0.0), axis=1, keepdims=True)
    lanes = lax.broadcasted_iota(jnp.int32, (1, width), 1)
    first = lanes < width // 2
    place = jnp.where(first, row_col, col_col)
    embed = jnp.sin(place * pos_tab[0:1, :] + pos_tab[1:2, :])
    loads[3].wait()
    x_in = tok[...].astype(F32) + embed
    xin_s[...] = x_in
    centered = x_in - jnp.mean(x_in, axis=1, keepdims=True)
    variance = jnp.mean(centered * centered, axis=1, keepdims=True)
    norm_s[...] = centered * lax.rsqrt(variance + 1e-6)

    @pl.loop(1, n)
    def _(step):
        mod_copy(step, lax.rem(me - step + n, n)).wait_recv()

    @pl.loop(1, n)
    def _(step):
        gate_copy(step, me).start()

    modulation = jnp.sum(mods[...].astype(F32), axis=0)
    shift = modulation[0:1]
    scale = modulation[1:2]
    modulated = (norm_s[...] * (1.0 + scale) + shift).astype(BF16)
    loads[4].wait()
    spare = jnp.zeros((rows, send.shape[2] - 3 * head), BF16)
    part_heads = HEADS // 2

    def pair_copy(to, slot):
        return pltpu.make_async_remote_copy(
            src_ref=send.at[lax.rem(to, HEADS)],
            dst_ref=got.at[slot],
            send_sem=psend.at[to],
            recv_sem=precv.at[slot],
            device_id={"patch": to},
            device_id_type=MESH,
        )

    def make_half(half):
        low = half * part_heads * head
        start = low // 128 * 128
        stop = -(-(low + part_heads * head) // 128) * 128
        parts = [
            dot(modulated, qkv[:, i * width + start : i * width + stop]).astype(BF16)
            for i in range(3)
        ]
        for h in range(part_heads):
            cols = slice(low - start + h * head, low - start + (h + 1) * head)
            send[half * part_heads + h] = jnp.concatenate(
                [part[:, cols] for part in parts] + [spare], axis=1
            )

        @pl.loop(0, groups * part_heads)
        def _(j):
            turn = lax.rem(me + j, part_heads)
            to = (j // part_heads) * HEADS + half * part_heads + turn

            @pl.when(to != me)
            def _():
                pair_copy(to, me).start()

    @pl.when(my_head < part_heads)
    def _():
        make_half(1)
        make_half(0)

    @pl.when(my_head >= part_heads)
    def _():
        make_half(0)
        make_half(1)

    got[me] = send[my_head]
    tail = lax.broadcasted_iota(jnp.int32, (chunk, vbuf.shape[1] - head), 1)
    ones = jnp.where(tail == 0, 1.0, 0.0).astype(BF16)
    slot_ids = lax.broadcasted_iota(jnp.int32, (rows, 1), 0)
    lane_ids = lax.broadcasted_iota(jnp.int32, (rows, kbuf.shape[1]), 1)
    for g in range(groups):
        vbuf[g * chunk : (g + 1) * chunk, head:] = ones
    for b in range(n):
        bias = jnp.where(slot_ids < counts[b], 0.0, NEG)
        kbuf[b * rows : (b + 1) * rows, :] = jnp.where(lane_ids == head, bias, 0.0).astype(BF16)

    @pl.loop(1, n)
    def _(step):
        pair_copy(me, lax.rem(me - step + n, n)).wait_recv()

    for g in range(groups):
        block = got[g * HEADS : (g + 1) * HEADS].reshape(chunk, got.shape[2])
        kbuf[g * chunk : (g + 1) * chunk, :head] = block[:, head : 2 * head]
        vbuf[g * chunk : (g + 1) * chunk, :head] = block[:, 2 * head : 3 * head]


    def att_copy(j, slot, to):
        return pltpu.make_async_remote_copy(
            src_ref=att.at[j],
            dst_ref=back.at[slot],
            send_sem=asend.at[j],
            recv_sem=arecv.at[slot],
            device_id={"patch": group * HEADS + to},
            device_id_type=MESH,
        )

    pairs = HEADS // 4
    mine = my_head // pairs

    @pl.loop(0, HEADS // pairs)
    def _(step):
        base = lax.rem(mine // 2 + 1 + step // 2, 2) * 2 + lax.rem(mine + 1 + step, 2)
        base = base * pairs
        block = got[pl.ds(group * HEADS + base, pairs)].reshape(pairs * rows, got.shape[2])
        query = jnp.concatenate(
            [block[:, :head], jnp.ones((pairs * rows, 1), BF16)], axis=1
        )
        query = jnp.concatenate(
            [query, jnp.zeros((pairs * rows, kbuf.shape[1] - head - 1), BF16)], axis=1
        )
        top = weighted = None
        for g in range(groups):
            keys = kbuf[g * chunk : (g + 1) * chunk, :]
            scores = lax.dot_general(
                query, keys, (((1,), (1,)), ((), ())), preferred_element_type=F32
            )
            new_top = jnp.max(scores, axis=1, keepdims=True)
            if g:
                new_top = jnp.maximum(top, new_top)
            prob = jnp.exp2((scores - new_top) * inv_root).astype(BF16)
            mixed = dot(prob, vbuf[g * chunk : (g + 1) * chunk, :])
            if g:
                mixed = weighted * jnp.exp2((top - new_top) * inv_root) + mixed
            top, weighted = new_top, mixed
        total = weighted[:, head : head + 1]
        result = weighted / total
        for i in range(pairs):
            att[base + i] = fold(result[i * rows : (i + 1) * rows, :head]).astype(BF16)
        for i in range(pairs):

            @pl.when(base + i != my_head)
            def _():
                att_copy(base + i, my_head, base + i).start()

    back[my_head] = att[my_head]
    filler = jnp.zeros((rows, ow.shape[1] - head), F32)
    for load in ow_loads:
        load.wait()

    @pl.loop(1, n)
    def _(step):
        gate_copy(step, lax.rem(me - step + n, n)).wait_recv()

    gate_rows = jnp.sum(gates[...].astype(F32), axis=0)
    gate = jnp.concatenate([gate_rows[0:1], gate_rows[1:2, 2 * span - width :]], axis=1)

    @pl.loop(1, n)
    def _(step):
        mod_copy(step, me).wait_send()
        pair_copy(lax.rem(me + step, n), me).wait_send()
        gate_copy(step, me).wait_send()

    @pl.loop(1, HEADS)
    def _(step):
        other = lax.rem(my_head + step, HEADS)
        att_copy(other, other, other).wait_recv()

    attended = jnp.concatenate(
        [
            piece
            for h in range(HEADS)
            for piece in (unfold(back[h].astype(F32), rows, head - 64), filler)
        ],
        axis=1,
    ).astype(BF16)
    weight = ow[...].reshape(HEADS * ow.shape[1], width)
    valid = (lax.broadcasted_iota(jnp.int32, (rows, 1), 0) < counts[me]).astype(F32)
    cut = width // 256 * 128
    stores = []
    for i, cols in enumerate([slice(0, cut), slice(cut, width)]):
        projected = dot(attended, weight[:, cols])
        done[:, cols] = (xin_s[:, cols] + gate[:, cols] * projected * valid).astype(BF16)
        stores.append(pltpu.make_async_copy(done.at[:, cols], out.at[:, cols], osem.at[i]))
        stores[-1].start()

    @pl.loop(1, HEADS)
    def _(step):
        other = lax.rem(my_head + step, HEADS)
        att_copy(other, other, other).wait_send()

    for store in stores:
        store.wait()


def tables(width, freq):
    quarter, half = width // 4, freq // 2
    omega = np.power(10000.0, -np.arange(quarter) / quarter)
    turn = math.pi / 2
    pos_tab = np.stack([np.tile(omega, 4), np.repeat([0.0, turn, 0.0, turn], quarter)])
    wave = np.exp(-math.log(10000.0) * np.arange(half) / half)
    time_tab = np.stack([np.tile(wave, 2), np.repeat([turn, 0.0], half)])
    return pos_tab.astype(np.float32), time_tab.astype(np.float32)


def per_device(
    tokens, positions, counts, timestep, time_in, time_out, ada_weight, qkv_weight, out_weight
):
    n = lax.axis_size("patch")
    rows, width = tokens.shape
    head = width // HEADS
    lane = 128
    head_pad = -(-head // lane) * lane
    pack = -(-3 * head // lane) * lane
    fold_back = rows // 2 + fold_group(rows, head - 64)
    pos_tab, time_tab = tables(width, time_in.shape[0])
    smem = pl.BlockSpec(memory_space=pltpu.SMEM)
    vmem = pl.BlockSpec(memory_space=pltpu.VMEM)
    hbm = pl.BlockSpec(memory_space=pl.ANY)
    result = pl.pallas_call(
        functools.partial(block_kernel, n, rows, width, head),
        out_shape=jax.ShapeDtypeStruct((rows, width), BF16),
        in_specs=[smem, smem, vmem, vmem, vmem] + [hbm] * 6,
        out_specs=hbm,
        scratch_shapes=[
            pltpu.VMEM(tokens.shape, BF16),
            pltpu.VMEM(time_in.shape, BF16),
            pltpu.VMEM(time_out.shape[::-1], BF16),
            pltpu.VMEM(ada_weight.shape, BF16),
            pltpu.VMEM(qkv_weight.shape, BF16),
            pltpu.VMEM((HEADS, head_pad, width), BF16),
            pltpu.VMEM((n, 2, width), BF16),
            pltpu.VMEM((n, 2, -(-width // 256) * 128), BF16),
            pltpu.VMEM((rows, width), F32),
            pltpu.VMEM((rows, width), F32),
            pltpu.VMEM((HEADS, rows, pack), BF16),
            pltpu.VMEM((n, rows, pack), BF16),
            pltpu.VMEM((n * rows, head_pad), BF16),
            pltpu.VMEM((n * rows, head_pad), BF16),
            pltpu.VMEM((HEADS, fold_back, lane), BF16),
            pltpu.VMEM((HEADS, fold_back, lane), BF16),
            pltpu.VMEM((rows, width), BF16),
            pltpu.SemaphoreType.DMA((2,)),
            pltpu.SemaphoreType.DMA((5,)),
            pltpu.SemaphoreType.DMA((HEADS,)),
            pltpu.SemaphoreType.DMA((n,)),
            pltpu.SemaphoreType.DMA((n,)),
            pltpu.SemaphoreType.DMA((n,)),
            pltpu.SemaphoreType.DMA((n,)),
            pltpu.SemaphoreType.DMA((n,)),
            pltpu.SemaphoreType.DMA((n,)),
            pltpu.SemaphoreType.DMA((HEADS,)),
            pltpu.SemaphoreType.DMA((HEADS,)),
        ],
        compiler_params=pltpu.CompilerParams(
            collective_id=0, has_side_effects=True, vmem_limit_bytes=60 * 2**20
        ),
    )(
        counts, timestep, positions, pos_tab, time_tab,
        tokens, time_in, time_out.T, ada_weight, qkv_weight, out_weight,
    )
    return result


def solution(mesh):
    placed = (
        P(("req", "patch"), None),
        P(None, ("req", "patch")),
        P("req"),
        P("req"),
        P(),
        P(None, "patch"),
        P("patch", None),
        P(),
        P(),
    )
    return jax.shard_map(
        per_device, mesh=mesh, in_specs=placed, out_specs=P(("req", "patch"), None), check_vma=False
    )
```

profile of v0, /device:TPU:0, one launch (start us, length us, event | category | flops | bytes accessed | tf_op | source)
XLA Modules:
  0.0 33.9 jit_solution(1978166422979844664)
XLA Ops:
  0.7 31.6 %shard_map.109 = bf16[48,1152]{1,0:T(8,128)(2,1)} custom-call(s32[16]{0:T(128)} %counts.1, s32[1]{0:T(128)S(6)} %copy.13.tstep, s32[2,48]{1,0:T(2,128)} %pos.1, f32[2,1152]{1,0:T(2,128)} %constant.4.clone.pos_tab, f32[2,256]{1,0:T(2,128)} %constant.5.clone.time_tab, bf16[48,1152]{1,0:T(8,128)(2,1)} %tok_h.1, bf16[256,1152]{1,0:T(8,128)(2,1)} %tin_h.1, ...), custom_call_target="tpu_custom_call" | custom-call | tf_op jit(solution)/shard_map/pallas_call | solution.py:365
  32.3 1.6 %copy.14 = bf16[48,1152]{1,0:T(8,128)(2,1)} copy(bf16[48,1152]{1,0:T(8,128)(2,1)} %shard_map.109) | data formatting | bytes 221184
where the time goes:
time: 34.1 us; the launch traced here: 33.9 us
  Pallas kernels  31.6 us (93%)
  local copies, waits for them, and re-layouts  1.55 us (5%)
  between operations  0.66 us (2%)
    pallas_call x1, Pallas kernels, per_device(): pl.pallas_call(functools.partial(block_kernel, n, rows, width, head), out...  31.6 us
    unnamed x1, local copies, waits for them, and re-layouts  1.55 us

commit v1 on v0

--- a/solution.py
+++ b/solution.py
@@ -58,11 +58,11 @@
 
 def block_kernel(
     n, rows, width, head,
-    counts, tstep, pos, pos_tab, time_tab,
+    counts_h, tstep_h, pos_h, pos_tab_h, time_tab_h,
     tok_h, tin_h, tout_h, ada_h, qkv_h, ow_h,
     out,
-    tok, tin, tout, ada, qkv, ow, mods, gates, xin_s, norm_s, send, got, kbuf, vbuf, att, back,
-    done, osem, lsem, wsem, msend, mrecv, gsend, grecv, psend, precv, asend, arecv,
+    counts, tstep, pos, pos_tab, time_tab, tok, tin, tout, ada, qkv, ow, mods, gates, xin_s, norm_s, send, got, kbuf, vbuf, att, back,
+    lsem, ssem, wsem, msend, mrecv, gsend, grecv, psend, precv, asend, arecv,
 ):
     me = lax.axis_index("patch")
     my_head = lax.rem(me, HEADS)
@@ -73,6 +73,9 @@
 
     barrier = pltpu.get_barrier_semaphore()
 
+    def drain(ref, sem):
+        pltpu.make_async_copy(ref, ref, sem.at[0]).wait()
+
     @pl.loop(1, n)
     def _(step):
         pl.semaphore_signal(
@@ -85,8 +88,17 @@
             [(tin_h, tin), (tout_h, tout), (ada_h, ada), (tok_h, tok), (qkv_h, qkv)]
         )
     ]
-    for load in loads[:3]:
+    small = [
+        pltpu.make_async_copy(src, dst, ssem.at[i])
+        for i, (src, dst) in enumerate(
+            [(tstep_h, tstep), (time_tab_h, time_tab), (counts_h, counts),
+             (pos_h, pos), (pos_tab_h, pos_tab)]
+        )
+    ]
+    for load in small[:2] + loads[:4] + small[2:]:
         load.start()
+    for load in small[:2]:
+        load.wait()
 
     angles = tstep[0].astype(F32) * time_tab[0:1, :] + time_tab[1:2, :]
     features = jnp.sin(angles).astype(BF16)
@@ -105,8 +117,7 @@
     gates[me] = jnp.concatenate(
         [partial[:, 2 * width : 2 * width + span], partial[:, 3 * width - span :]], axis=0
     ).astype(BF16)
-    for load in loads[3:]:
-        load.start()
+    loads[4].start()
 
     pl.semaphore_wait(barrier, n - 1)
 
@@ -114,8 +125,8 @@
         return pltpu.make_async_remote_copy(
             src_ref=mods.at[slot],
             dst_ref=mods.at[slot],
-            send_sem=msend.at[step],
-            recv_sem=mrecv.at[slot],
+            send_sem=msend.at[0],
+            recv_sem=mrecv.at[0],
             device_id={"patch": lax.rem(me + step, n)},
             device_id_type=MESH,
         )
@@ -124,8 +135,8 @@
         return pltpu.make_async_remote_copy(
             src_ref=gates.at[slot],
             dst_ref=gates.at[slot],
-            send_sem=gsend.at[step],
-            recv_sem=grecv.at[slot],
+            send_sem=gsend.at[0],
+            recv_sem=grecv.at[0],
             device_id={"patch": lax.rem(me + step, n)},
             device_id_type=MESH,
         )
@@ -137,7 +148,7 @@
     ow[:, head:, :] = jnp.zeros((HEADS, ow.shape[1] - head, width), BF16)
     ow_loads = [
         pltpu.make_async_copy(
-            ow_h.at[pl.ds(h * head, head), :], ow.at[h, pl.ds(0, head), :], wsem.at[h]
+            ow_h.at[pl.ds(h * head, head), :], ow.at[h, pl.ds(0, head), :], wsem.at[0]
         )
         for h in range(HEADS)
     ]
@@ -146,6 +157,8 @@
 
     ids = lax.broadcasted_iota(jnp.int32, (rows, rows), 0)
     eye = ids == lax.broadcasted_iota(jnp.int32, (rows, rows), 1)
+    for load in small[2:]:
+        load.wait()
     posf = pos[...].astype(F32)
     row_col = jnp.sum(jnp.where(eye, posf[0:1, :], 0.0), axis=1, keepdims=True)
     col_col = jnp.sum(jnp.where(eye, posf[1:2, :], 0.0), axis=1, keepdims=True)
@@ -160,9 +173,7 @@
     variance = jnp.mean(centered * centered, axis=1, keepdims=True)
     norm_s[...] = centered * lax.rsqrt(variance + 1e-6)
 
-    @pl.loop(1, n)
-    def _(step):
-        mod_copy(step, lax.rem(me - step + n, n)).wait_recv()
+    drain(mods.at[pl.ds(0, n - 1)], mrecv)
 
     @pl.loop(1, n)
     def _(step):
@@ -180,8 +191,8 @@
         return pltpu.make_async_remote_copy(
             src_ref=send.at[lax.rem(to, HEADS)],
             dst_ref=got.at[slot],
-            send_sem=psend.at[to],
-            recv_sem=precv.at[slot],
+            send_sem=psend.at[0],
+            recv_sem=precv.at[0],
             device_id={"patch": to},
             device_id_type=MESH,
         )
@@ -230,9 +241,7 @@
         bias = jnp.where(slot_ids < counts[b], 0.0, NEG)
         kbuf[b * rows : (b + 1) * rows, :] = jnp.where(lane_ids == head, bias, 0.0).astype(BF16)
 
-    @pl.loop(1, n)
-    def _(step):
-        pair_copy(me, lax.rem(me - step + n, n)).wait_recv()
+    drain(got.at[pl.ds(0, n - 1)], precv)
 
     for g in range(groups):
         block = got[g * HEADS : (g + 1) * HEADS].reshape(chunk, got.shape[2])
@@ -244,8 +253,8 @@
         return pltpu.make_async_remote_copy(
             src_ref=att.at[j],
             dst_ref=back.at[slot],
-            send_sem=asend.at[j],
-            recv_sem=arecv.at[slot],
+            send_sem=asend.at[0],
+            recv_sem=arecv.at[0],
             device_id={"patch": group * HEADS + to},
             device_id_type=MESH,
         )
@@ -290,26 +299,17 @@
 
     back[my_head] = att[my_head]
     filler = jnp.zeros((rows, ow.shape[1] - head), F32)
-    for load in ow_loads:
-        load.wait()
-
-    @pl.loop(1, n)
-    def _(step):
-        gate_copy(step, lax.rem(me - step + n, n)).wait_recv()
+    pltpu.make_async_copy(ow_h, ow_h, wsem.at[0]).wait()
+
+    drain(gates.at[pl.ds(0, n - 1)], grecv)
 
     gate_rows = jnp.sum(gates[...].astype(F32), axis=0)
     gate = jnp.concatenate([gate_rows[0:1], gate_rows[1:2, 2 * span - width :]], axis=1)
 
-    @pl.loop(1, n)
-    def _(step):
-        mod_copy(step, me).wait_send()
-        pair_copy(lax.rem(me + step, n), me).wait_send()
-        gate_copy(step, me).wait_send()
-
-    @pl.loop(1, HEADS)
-    def _(step):
-        other = lax.rem(my_head + step, HEADS)
-        att_copy(other, other, other).wait_recv()
+    drain(mods.at[pl.ds(0, n - 1)], msend)
+    drain(gates.at[pl.ds(0, n - 1)], gsend)
+    drain(got.at[pl.ds(0, n - 1)], psend)
+    drain(back.at[pl.ds(0, HEADS - 1)], arecv)
 
     attended = jnp.concatenate(
         [
@@ -322,20 +322,11 @@
     weight = ow[...].reshape(HEADS * ow.shape[1], width)
     valid = (lax.broadcasted_iota(jnp.int32, (rows, 1), 0) < counts[me]).astype(F32)
     cut = width // 256 * 128
-    stores = []
     for i, cols in enumerate([slice(0, cut), slice(cut, width)]):
         projected = dot(attended, weight[:, cols])
-        done[:, cols] = (xin_s[:, cols] + gate[:, cols] * projected * valid).astype(BF16)
-        stores.append(pltpu.make_async_copy(done.at[:, cols], out.at[:, cols], osem.at[i]))
-        stores[-1].start()
-
-    @pl.loop(1, HEADS)
-    def _(step):
-        other = lax.rem(my_head + step, HEADS)
-        att_copy(other, other, other).wait_send()
-
-    for store in stores:
-        store.wait()
+        out[:, cols] = (xin_s[:, cols] + gate[:, cols] * projected * valid).astype(BF16)
+
+    drain(back.at[pl.ds(0, HEADS - 1)], asend)
 
 
 def tables(width, freq):
@@ -364,10 +355,15 @@
     hbm = pl.BlockSpec(memory_space=pl.ANY)
     result = pl.pallas_call(
         functools.partial(block_kernel, n, rows, width, head),
-        out_shape=jax.ShapeDtypeStruct((rows, width), BF16),
-        in_specs=[smem, smem, vmem, vmem, vmem] + [hbm] * 6,
-        out_specs=hbm,
+        out_shape=pltpu.VMEM((rows, width), BF16),
+        in_specs=[hbm] * 11,
+        out_specs=vmem,
         scratch_shapes=[
+            pltpu.SMEM(counts.shape, jnp.int32),
+            pltpu.SMEM(timestep.shape, jnp.int32),
+            pltpu.VMEM(positions.shape, jnp.int32),
+            pltpu.VMEM(pos_tab.shape, F32),
+            pltpu.VMEM(time_tab.shape, F32),
             pltpu.VMEM(tokens.shape, BF16),
             pltpu.VMEM(time_in.shape, BF16),
             pltpu.VMEM(time_out.shape[::-1], BF16),
@@ -384,18 +380,17 @@
             pltpu.VMEM((n * rows, head_pad), BF16),
             pltpu.VMEM((HEADS, fold_back, lane), BF16),
             pltpu.VMEM((HEADS, fold_back, lane), BF16),
-            pltpu.VMEM((rows, width), BF16),
-            pltpu.SemaphoreType.DMA((2,)),
             pltpu.SemaphoreType.DMA((5,)),
-            pltpu.SemaphoreType.DMA((HEADS,)),
-            pltpu.SemaphoreType.DMA((n,)),
-            pltpu.SemaphoreType.DMA((n,)),
-            pltpu.SemaphoreType.DMA((n,)),
-            pltpu.SemaphoreType.DMA((n,)),
-            pltpu.SemaphoreType.DMA((n,)),
-            pltpu.SemaphoreType.DMA((n,)),
-            pltpu.SemaphoreType.DMA((HEADS,)),
-            pltpu.SemaphoreType.DMA((HEADS,)),
+            pltpu.SemaphoreType.DMA((5,)),
+            pltpu.SemaphoreType.DMA((1,)),
+            pltpu.SemaphoreType.DMA((1,)),
+            pltpu.SemaphoreType.DMA((1,)),
+            pltpu.SemaphoreType.DMA((1,)),
+            pltpu.SemaphoreType.DMA((1,)),
+            pltpu.SemaphoreType.DMA((1,)),
+            pltpu.SemaphoreType.DMA((1,)),
+            pltpu.SemaphoreType.DMA((1,)),
+            pltpu.SemaphoreType.DMA((1,)),
         ],
         compiler_params=pltpu.CompilerParams(
             collective_id=0, has_side_effects=True, vmem_limit_bytes=60 * 2**20

time: 34.1 us -> 30.4 us (0.89)
  Pallas kernels: 31.6 us -> 28.9 us
  local copies, waits for them, and re-layouts: 1.55 us -> 0.65 us
    pallas_call x1, Pallas kernels: 31.6 us -> 28.9 us  [per_device(): pl.pallas_call(functools.partial(block_kernel, n, rows, width, head), out...]
    unnamed x1, local copies, waits for them, and re-layouts: 1.55 us -> 0.65 us
where the time goes in v1:
time: 30.4 us; the launch traced here: 30.2 us
  Pallas kernels  28.9 us (95%)
  between operations  0.66 us (2%)
  local copies, waits for them, and re-layouts  0.65 us (2%)
    pallas_call x1, Pallas kernels, per_device(): pl.pallas_call(functools.partial(block_kernel, n, rows, width, head), out...  28.9 us
    unnamed x1, local copies, waits for them, and re-layouts  0.65 us

profile of v1, /device:TPU:0, one launch (start us, length us, event | category | flops | bytes accessed | tf_op | source)
XLA Modules:
  0.0 30.2 jit_solution(4962136589006859251)
XLA Ops:
  0.7 28.9 %shard_map.109 = bf16[48,1152]{1,0:T(8,128)(2,1)S(1)} custom-call(s32[16]{0:T(128)} %counts_h.1, s32[1]{0:T(128)S(6)} %copy.14.tstep_h, s32[2,48]{1,0:T(2,128)} %pos_h.1, f32[2,1152]{1,0:T(2,128)} %constant.4.clone.pos_tab_h, f32[2,256]{1,0:T(2,128)} %constant.5.clone.time_tab_h, bf16[48,1152]{1,0:T(8,128)(2,1)} %tok_h.1, bf16[256,1152]{1,0:T(8,128)(2,1)} %tin_h.1, ...), custom_call_target="tpu_custom_call" | custom-call | tf_op jit(solution)/shard_map/pallas_call | solution.py:356
  29.6 0.6 %copy.13 = bf16[48,1152]{1,0:T(8,128)(2,1)} copy(bf16[48,1152]{1,0:T(8,128)(2,1)S(1)} %shard_map.109) | data formatting | bytes 221184

commit v2 on v1

v2 whole, which is shorter than its diff:
```python
import functools
import math

import jax
import jax.numpy as jnp
import numpy as np
from jax import lax
from jax.experimental import pallas as pl
from jax.experimental.pallas import tpu as pltpu
from jax.sharding import PartitionSpec as P

HEADS = 16
PAIRS = HEADS // 2
LANE = 128
NEG = -1e30
F32 = jnp.float32
BF16 = jnp.bfloat16
MESH = pl.DeviceIdType.MESH
PI_PARTS = (3.140625, 0.000967502593994140625, 1.509957990978376432e-07)


def silu(v):
    return v / (1.0 + jnp.exp(-v))


def sine(x):
    turns = jnp.floor(x * (1.0 / math.pi) + 0.5)
    r = x - turns * PI_PARTS[0]
    r = r - turns * PI_PARTS[1]
    r = r - turns * PI_PARTS[2]
    s = r * r
    poly = -2.3889859e-08 * s + 2.7525562e-06
    poly = poly * s - 0.00019840874
    poly = poly * s + 0.0083333310
    poly = poly * s - 0.16666667
    value = r + r * (s * poly)
    odd = turns - 2.0 * jnp.floor(turns * 0.5)
    return value * (1.0 - 2.0 * odd)


def dot(a, b):
    return jnp.dot(a, b, preferred_element_type=F32)


def dot_t(a, b):
    return lax.dot_general(a, b, (((1,), (1,)), ((), ())), preferred_element_type=F32)


def one_row_dot(row, matrix):
    wide = jnp.broadcast_to(row, (16, row.shape[1])).astype(BF16)
    return dot(wide, matrix)[0:1]


def fold_rows(rows, stride):
    group = 8
    while rows % group or rows // group * stride > LANE:
        group += 8
    return group


def turned(x, shift):
    shift %= LANE
    return pltpu.roll(x, shift, axis=1) if shift else x


def fold(blocks, base, group, stride, ex, at):
    lanes = lax.broadcasted_iota(jnp.int32, (group, LANE), 1)
    packed = base
    for r in range(blocks[0].shape[0] // group):
        for j, block in enumerate(blocks):
            low = r * stride + j * ex
            piece = turned(block[r * group : (r + 1) * group], low - at)
            packed = jnp.where((lanes >= low) & (lanes < low + ex), piece, packed)
    return packed


def unfold(packed, rows, stride, to):
    group = packed.shape[0]
    return jnp.concatenate(
        [turned(packed, to - r * stride) for r in range(rows // group)], axis=0
    )


def block_kernel(
    n, rows, width, head,
    counts_h, tstep_h, pos_h, pos_tab_h, time_tab_h,
    tok_h, tin_h, tout_h, ada_h, qkv_h, ow_h,
    out,
    counts, tstep, pos, pos_tab, time_tab, tok, tin, tout, ada, qkv, ow, mods, gates,
    xin_s, norm_s, nsend, ngot, send0, send1, got0, got1, o_s, top_s, att, back,
    lsem, ssem, wsem, msend, mrecv, gsend, grecv, nsem, nrecv, psend, precv, rsend, rrecv,
    asend, arecv,
):
    me = lax.axis_index("patch")
    pair = lax.rem(me, PAIRS)
    side = lax.rem(me // PAIRS, 2)
    group = me // HEADS
    groups = n // HEADS
    mirror = me + PAIRS * (1 - 2 * side)
    ex = 2 * head - LANE
    stride0, stride1 = 3 * ex + 2, 2 * ex + 2
    fold0, fold1, fold2 = fold_rows(rows, stride0), fold_rows(rows, stride1), fold_rows(rows, ex)
    scale_q = math.log2(math.e) / math.sqrt(head)

    barrier = pltpu.get_barrier_semaphore()

    def drain(ref, sem):
        pltpu.make_async_copy(ref, ref, sem.at[0]).wait()

    def remote(src, dst, send, recv, to):
        return pltpu.make_async_remote_copy(
            src_ref=src, dst_ref=dst, send_sem=send.at[0], recv_sem=recv.at[0],
            device_id={"patch": to}, device_id_type=MESH,
        )

    @pl.loop(1, n)
    def _(step):
        pl.semaphore_signal(
            barrier, inc=1, device_id={"patch": lax.rem(me + step, n)}, device_id_type=MESH
        )

    loads = [
        pltpu.make_async_copy(src, dst, lsem.at[i])
        for i, (src, dst) in enumerate(
            [(tin_h, tin), (tout_h, tout), (ada_h, ada), (tok_h, tok), (qkv_h, qkv)]
        )
    ]
    small = [
        pltpu.make_async_copy(src, dst, ssem.at[i])
        for i, (src, dst) in enumerate(
            [(tstep_h, tstep), (time_tab_h, time_tab), (counts_h, counts),
             (pos_h, pos), (pos_tab_h, pos_tab)]
        )
    ]
    for load in small[:2] + loads[:4] + small[2:]:
        load.start()
    for load in small[:2]:
        load.wait()

    angles = tstep[0].astype(F32) * time_tab[0:1, :] + time_tab[1:2, :]
    features = sine(angles).astype(BF16)
    loads[0].wait()
    hidden = silu(one_row_dot(features, tin[...])).astype(BF16)
    loads[1].wait()
    wide = jnp.broadcast_to(hidden, (16, width))
    cond = dot_t(wide, tout[...])
    activated = silu(cond[0:1]).astype(BF16)
    loads[2].wait()
    partial = one_row_dot(activated, ada[...])
    mods[me] = jnp.concatenate(
        [partial[:, :width], partial[:, width : 2 * width]], axis=0
    ).astype(BF16)
    span = gates.shape[2]
    gates[me] = jnp.concatenate(
        [partial[:, 2 * width : 2 * width + span], partial[:, 3 * width - span :]], axis=0
    ).astype(BF16)
    loads[4].start()
    ow_load = pltpu.make_async_copy(ow_h, ow, wsem.at[0])
    ow_load.start()

    pl.semaphore_wait(barrier, n - 1)

    @pl.loop(1, n)
    def _(step):
        remote(mods.at[me], mods.at[me], msend, mrecv, lax.rem(me + step, n)).start()

    ids = lax.broadcasted_iota(jnp.int32, (rows, rows), 0)
    eye = ids == lax.broadcasted_iota(jnp.int32, (rows, rows), 1)
    for load in small[2:]:
        load.wait()
    posf = pos[...].astype(F32)
    row_col = jnp.sum(jnp.where(eye, posf[0:1, :], 0.0), axis=1, keepdims=True)
    col_col = jnp.sum(jnp.where(eye, posf[1:2, :], 0.0), axis=1, keepdims=True)
    wide_lanes = lax.broadcasted_iota(jnp.int32, (1, width), 1)
    place = jnp.where(wide_lanes < width // 2, row_col, col_col)
    embed = sine(place * pos_tab[0:1, :] + pos_tab[1:2, :])
    loads[3].wait()
    x_in = tok[...].astype(F32) + embed
    xin_s[...] = x_in
    centered = x_in - jnp.mean(x_in, axis=1, keepdims=True)
    variance = jnp.mean(centered * centered, axis=1, keepdims=True)
    norm = centered * lax.rsqrt(variance + 1e-6)
    norm_s[...] = norm
    nsend[...] = norm.astype(BF16)
    mirror_copy = remote(nsend, ngot, nsem, nrecv, mirror)
    mirror_copy.start()

    drain(mods.at[pl.ds(0, n - 1)], mrecv)
    modulation = jnp.sum(mods[...].astype(F32), axis=0)
    shift = modulation[0:1]
    gain = 1.0 + modulation[1:2]
    modulated = (norm_s[...] * gain + shift).astype(BF16)
    loads[4].wait()

    lane_ids = lax.broadcasted_iota(jnp.int32, (rows, LANE), 1)

    def base_of(owner, fold_group, stride, blocks):
        lanes = lax.broadcasted_iota(jnp.int32, (fold_group, LANE), 1)
        slot = lax.broadcasted_iota(jnp.int32, (fold_group, LANE), 0)
        base = jnp.zeros((fold_group, LANE), F32)
        for r in range(rows // fold_group):
            low = r * stride + blocks * ex
            base = jnp.where(lanes == low, 1.0, base)
            bias = jnp.where(slot + r * fold_group < counts[owner], 0.0, NEG)
            base = jnp.where(lanes == low + 1, bias, base)
        return base

    def project(first, x):
        return [dot(x, qkv[:, i * width : (i + 1) * width]) for i in range(first, 3)]

    def pack(parts, base, fold_group, stride, buffer):
        for p in range(PAIRS):
            low, cut = p * LANE, p * ex
            nexts = []
            for j, part in enumerate(parts):
                here = part[:, low : low + LANE]
                after = part[:, low + LANE : low + 2 * LANE]
                nexts.append(after)
                mixed = jnp.where(lane_ids < cut, after, here) if cut else here
                buffer[p, j * rows : (j + 1) * rows, :] = mixed.astype(BF16)
            packed = fold(nexts, base, fold_group, stride, ex, cut)
            buffer[p, len(parts) * rows :, :] = packed.astype(BF16)

    def spread(buffer, got, send, recv):
        slot = group * PAIRS + pair

        @pl.loop(1, groups * PAIRS)
        def _(j):
            turn = lax.rem(slot + j, groups * PAIRS)
            to = turn // PAIRS * HEADS + side * PAIRS + lax.rem(turn, PAIRS)
            remote(buffer.at[lax.rem(turn, PAIRS)], got.at[slot], send, recv, to).start()

        got[slot] = buffer[pair]

    parts = project(0, modulated)
    pack([parts[0] * scale_q] + parts[1:], base_of(me, fold0, stride0, 3), fold0, stride0, send0)
    spread(send0, got0, psend, precv)

    @pl.loop(1, n)
    def _(step):
        remote(gates.at[me], gates.at[me], gsend, grecv, lax.rem(me + step, n)).start()

    mirror_copy.wait_recv()
    modulated = (ngot[...].astype(F32) * gain + shift).astype(BF16)
    pack(project(1, modulated), base_of(mirror, fold1, stride1, 2), fold1, stride1, send1)
    spread(send1, got1, rsend, rrecv)

    slots = groups * PAIRS
    drain(got0.at[pl.ds(0, slots - 1)], precv)

    def keys_of(got, g, first, fold_group, stride, to):
        block = got[g * PAIRS : (g + 1) * PAIRS]
        cells = PAIRS * rows
        k = block[:, first * rows : (first + 1) * rows].reshape(cells, LANE)
        v = block[:, (first + 1) * rows : (first + 2) * rows].reshape(cells, LANE)
        extra = jnp.concatenate(
            [unfold(block[s, (first + 2) * rows :].astype(F32), rows, stride, to) for s in range(PAIRS)],
            axis=0,
        ).astype(BF16)
        return jnp.concatenate([k, extra], axis=1), jnp.concatenate([v, extra], axis=1)

    half = PAIRS // 2
    cells = half * rows
    near = pair // half
    q_lanes = lax.broadcasted_iota(jnp.int32, (cells, LANE), 1)
    column = lax.rem(q_lanes + (LANE - ex * pair), LANE)
    first_head = column < head
    bias_one = jnp.where(q_lanes == 3 * ex + 1, 1.0, 0.0)

    def queries_of(base):
        block = got0[pl.ds(group * PAIRS + base, half)]
        qa = block[:, :rows].reshape(cells, LANE).astype(F32)
        extra = jnp.concatenate(
            [
                unfold(block[s, 3 * rows :].astype(F32), rows, stride0, ex)
                for s in range(half)
            ],
            axis=0,
        )
        extra = jnp.where((q_lanes >= ex) & (q_lanes < 2 * ex), extra, bias_one)
        top = jnp.concatenate([jnp.where(first_head, qa, 0.0), bias_one], axis=1)
        low = jnp.concatenate([jnp.where(first_head, 0.0, qa), extra], axis=1)
        return jnp.concatenate([top, low], axis=0).astype(BF16)

    bases = [(1 - near) * half, near * half]
    queries = [queries_of(base) for base in bases]

    def attend(i, keys, values, first):
        scores = dot_t(queries[i], keys)
        top = jnp.max(scores, axis=1, keepdims=True)
        if not first:
            before = top_s[i][:, 0:1]
            top = jnp.maximum(top, before)
        prob = jnp.exp2(scores - top).astype(BF16)
        mixed = dot(prob, values)
        if not first:
            mixed = o_s[i] * jnp.exp2(before - top) + mixed
        return top, mixed

    def keep(i, state):
        top_s[i] = jnp.broadcast_to(state[0], top_s.shape[1:])
        o_s[i] = state[1]

    for g in range(groups):
        keys, values = keys_of(got0, g, 1, fold0, stride0, 0)
        for i in range(2):
            keep(i, attend(i, keys, values, g == 0))

    drain(got1.at[pl.ds(0, slots - 1)], rrecv)
    for g in range(groups - 1):
        keys, values = keys_of(got1, g, 0, fold1, stride1, ex)
        for i in range(2):
            keep(i, attend(i, keys, values, False))

    keys, values = keys_of(got1, groups - 1, 0, fold1, stride1, ex)
    fold_zero = jnp.zeros((fold2, LANE), F32)
    for i in range(2):
        _, mixed = attend(i, keys, values, False)
        share = 1.0 / mixed[:, LANE + 3 * ex : LANE + 3 * ex + 1]
        mixed = mixed * share
        main = jnp.where(first_head, mixed[:cells, :LANE], mixed[cells:, :LANE])
        extra = mixed[cells:, LANE:]
        for s in range(half):
            span_s = slice(s * rows, (s + 1) * rows)
            slot = bases[i] + s
            att[slot, :rows, :] = main[span_s].astype(BF16)
            att[slot, rows:, :] = fold(
                [extra[span_s]], fold_zero, fold2, ex, ex, 2 * ex
            ).astype(BF16)
        for s in range(half):
            slot = bases[i] + s

            @pl.when(slot != pair)
            def _():
                remote(
                    att.at[slot], back.at[pair], asend, arecv, me - pair + slot
                ).start()

    back[pair] = att[pair]
    ow_load.wait()
    drain(gates.at[pl.ds(0, n - 1)], grecv)
    gate_rows = jnp.sum(gates[...].astype(F32), axis=0)
    gate = jnp.concatenate([gate_rows[0:1], gate_rows[1:2, 2 * span - width :]], axis=1)
    valid = (lax.broadcasted_iota(jnp.int32, (rows, 1), 0) < counts[me]).astype(F32)

    drain(mods.at[pl.ds(0, n - 1)], msend)
    drain(gates.at[pl.ds(0, n - 1)], gsend)
    mirror_copy.wait_send()
    drain(got0.at[pl.ds(0, slots - 1)], psend)
    drain(got1.at[pl.ds(0, slots - 1)], rsend)
    drain(back.at[pl.ds(0, PAIRS - 1)], arecv)

    rest = jnp.zeros((rows, LANE), F32)
    for p in range(PAIRS):
        piece = unfold(back[p, rows:, :].astype(F32), rows, ex, p * ex)
        rest = jnp.where((lane_ids >= p * ex) & (lane_ids < (p + 1) * ex), piece, rest)
    chunks = []
    for c in range(PAIRS + 1):
        here = back[c, :rows, :].astype(F32) if c < PAIRS else rest
        if c:
            here = jnp.where(lane_ids < c * ex, rest, here)
            here = jnp.where(lane_ids < (c - 1) * ex, back[c - 1, :rows, :].astype(F32), here)
        chunks.append(here)
    attended = jnp.concatenate(chunks, axis=1).astype(BF16)
    projected = dot(attended, ow[...])
    out[...] = (xin_s[...] + gate * projected * valid).astype(BF16)
    drain(back.at[pl.ds(0, PAIRS - 1)], asend)


def tables(width, freq):
    quarter, half = width // 4, freq // 2
    omega = np.power(10000.0, -np.arange(quarter) / quarter)
    turn = math.pi / 2
    pos_tab = np.stack([np.tile(omega, 4), np.repeat([0.0, turn, 0.0, turn], quarter)])
    wave = np.exp(-math.log(10000.0) * np.arange(half) / half)
    time_tab = np.stack([np.tile(wave, 2), np.repeat([turn, 0.0], half)])
    return pos_tab.astype(np.float32), time_tab.astype(np.float32)


def per_device(
    tokens, positions, counts, timestep, time_in, time_out, ada_weight, qkv_weight, out_weight
):
    n = lax.axis_size("patch")
    rows, width = tokens.shape
    head = width // HEADS
    ex = 2 * head - LANE
    assert 0 < ex and PAIRS * ex <= LANE and n % HEADS == 0
    size0 = 3 * rows + fold_rows(rows, 3 * ex + 2)
    size1 = 2 * rows + fold_rows(rows, 2 * ex + 2)
    size2 = rows + fold_rows(rows, ex)
    slots = n // 2
    queries = PAIRS * rows
    pos_tab, time_tab = tables(width, time_in.shape[0])
    hbm = pl.BlockSpec(memory_space=pl.ANY)
    vmem = pl.BlockSpec(memory_space=pltpu.VMEM)
    dma = pltpu.SemaphoreType.DMA
    return pl.pallas_call(
        functools.partial(block_kernel, n, rows, width, head),
        out_shape=pltpu.VMEM((rows, width), BF16),
        in_specs=[hbm] * 11,
        out_specs=vmem,
        scratch_shapes=[
            pltpu.SMEM(counts.shape, jnp.int32),
            pltpu.SMEM(timestep.shape, jnp.int32),
            pltpu.VMEM(positions.shape, jnp.int32),
            pltpu.VMEM(pos_tab.shape, F32),
            pltpu.VMEM(time_tab.shape, F32),
            pltpu.VMEM(tokens.shape, BF16),
            pltpu.VMEM(time_in.shape, BF16),
            pltpu.VMEM(time_out.shape[::-1], BF16),
            pltpu.VMEM(ada_weight.shape, BF16),
            pltpu.VMEM(qkv_weight.shape, BF16),
            pltpu.VMEM(out_weight.shape, BF16),
            pltpu.VMEM((n, 2, width), BF16),
            pltpu.VMEM((n, 2, -(-width // 256) * 128), BF16),
            pltpu.VMEM((rows, width), F32),
            pltpu.VMEM((rows, width), F32),
            pltpu.VMEM((rows, width), BF16),
            pltpu.VMEM((rows, width), BF16),
            pltpu.VMEM((PAIRS, size0, LANE), BF16),
            pltpu.VMEM((PAIRS, size1, LANE), BF16),
            pltpu.VMEM((slots, size0, LANE), BF16),
            pltpu.VMEM((slots, size1, LANE), BF16),
            pltpu.VMEM((2, queries, 2 * LANE), F32),
            pltpu.VMEM((2, queries, LANE), F32),
            pltpu.VMEM((PAIRS, size2, LANE), BF16),
            pltpu.VMEM((PAIRS, size2, LANE), BF16),
            dma((5,)),
            dma((5,)),
        ]
        + [dma((1,))] * 13,
        compiler_params=pltpu.CompilerParams(
            collective_id=0, has_side_effects=True, vmem_limit_bytes=60 * 2**20
        ),
    )(
        counts, timestep, positions, pos_tab, time_tab,
        tokens, time_in, time_out.T, ada_weight, qkv_weight, out_weight,
    )


def solution(mesh):
    placed = (
        P(("req", "patch"), None),
        P(None, ("req", "patch")),
        P("req"),
        P("req"),
        P(),
        P(None, "patch"),
        P("patch", None),
        P(),
        P(),
    )
    return jax.shard_map(
        per_device, mesh=mesh, in_specs=placed, out_specs=P(("req", "patch"), None), check_vma=False
    )
```

time: 30.4 us -> 28.4 us (0.934)
  Pallas kernels: 28.9 us -> 27 us
    pallas_call x1, Pallas kernels: 28.9 us -> 27 us  [per_device(): pl.pallas_call(functools.partial(block_kernel, n, rows, width, head), out...]
where the time goes in v2:
time: 28.4 us; the launch traced here: 28.3 us
  Pallas kernels  27 us (95%)
  between operations  0.66 us (2%)
  local copies, waits for them, and re-layouts  0.65 us (2%)
    pallas_call x1, Pallas kernels, per_device(): pl.pallas_call(functools.partial(block_kernel, n, rows, width, head), out...  27 us
    unnamed x1, local copies, waits for them, and re-layouts  0.65 us

profile of v2, /device:TPU:0, one launch (start us, length us, event | category | flops | bytes accessed | tf_op | source)
XLA Modules:
  0.0 28.3 jit_solution(2084449600897026229)
XLA Ops:
  0.7 27.0 %shard_map.109 = bf16[48,1152]{1,0:T(8,128)(2,1)S(1)} custom-call(s32[16]{0:T(128)} %counts_h.1, s32[1]{0:T(128)S(6)} %copy.14.tstep_h, s32[2,48]{1,0:T(2,128)} %pos_h.1, f32[2,1152]{1,0:T(2,128)} %constant.4.clone.pos_tab_h, f32[2,256]{1,0:T(2,128)} %constant.5.clone.time_tab_h, bf16[48,1152]{1,0:T(8,128)(2,1)} %tok_h.1, bf16[256,1152]{1,0:T(8,128)(2,1)} %tin_h.1, ...), custom_call_target="tpu_custom_call" | custom-call | tf_op jit(solution)/shard_map/pallas_call | solution.py:397
  27.6 0.6 %copy.13 = bf16[48,1152]{1,0:T(8,128)(2,1)} copy(bf16[48,1152]{1,0:T(8,128)(2,1)S(1)} %shard_map.109) | data formatting | bytes 221184

commit v3 on v2

--- a/solution.py
+++ b/solution.py
@@ -59,8 +59,14 @@
 
 
 def turned(x, shift):
-    shift %= LANE
-    return pltpu.roll(x, shift, axis=1) if shift else x
+    if isinstance(shift, int):
+        shift %= LANE
+        return pltpu.roll(x, shift, axis=1) if shift else x
+    return pltpu.roll(x, lax.rem(shift + LANE, LANE), axis=1)
+
+
+def flip(index, bit):
+    return index + bit * (1 - 2 * lax.rem(index // bit, 2))
 
 
 def fold(blocks, base, group, stride, ex, at):
@@ -86,10 +92,11 @@
     counts_h, tstep_h, pos_h, pos_tab_h, time_tab_h,
     tok_h, tin_h, tout_h, ada_h, qkv_h, ow_h,
     out,
-    counts, tstep, pos, pos_tab, time_tab, tok, tin, tout, ada, qkv, ow, mods, gates,
-    xin_s, norm_s, nsend, ngot, send0, send1, got0, got1, o_s, top_s, att, back,
-    lsem, ssem, wsem, msend, mrecv, gsend, grecv, nsem, nrecv, psend, precv, rsend, rrecv,
-    asend, arecv,
+    counts, tstep, pos, pos_tab, time_tab, tok, tin, tout, ada, near_w, far_w, kv_w, ow,
+    mods, gates, msum, mgot, gsum, ggot, xin_s, norm_s, nsend, ngot, xgot, zgot, sendd, sendp, send1, send2,
+    got0, got1, got2, o_s, top_s, att, back,
+    lsem, ssem, wsem, msend, mrecv, gsend, grecv, nsem, nrecv, dsend, drecv, psend, precv,
+    rsend, rrecv, tsend, trecv, asend, arecv, hsend, hrecv, fsend, frecv,
 ):
     me = lax.axis_index("patch")
     pair = lax.rem(me, PAIRS)
@@ -122,9 +129,24 @@
     loads = [
         pltpu.make_async_copy(src, dst, lsem.at[i])
         for i, (src, dst) in enumerate(
-            [(tin_h, tin), (tout_h, tout), (ada_h, ada), (tok_h, tok), (qkv_h, qkv)]
+            [(tin_h, tin), (tout_h, tout), (ada_h, ada), (tok_h, tok)]
         )
     ]
+    chip = pair // 2
+    far_chip = flip(flip(pair, 2), 4) // 2
+    reach = near_w.shape[1] // 3
+
+    def window(i, owner):
+        return pl.ds(pl.multiple_of(i * width + 2 * LANE * owner, LANE), reach)
+
+    qkv_loads = [
+        pltpu.make_async_copy(
+            qkv_h.at[:, window(i, owner)], dst.at[:, pl.ds(i * reach, reach)], wsem.at[k]
+        )
+        for k, (owner, dst) in ((1, (far_chip, far_w)), (2, (chip, near_w)))
+        for i in range(3)
+    ]
+    qkv_loads.insert(3, pltpu.make_async_copy(qkv_h.at[:, pl.ds(width, 2 * width)], kv_w, wsem.at[3]))
     small = [
         pltpu.make_async_copy(src, dst, ssem.at[i])
         for i, (src, dst) in enumerate(
@@ -147,22 +169,26 @@
     activated = silu(cond[0:1]).astype(BF16)
     loads[2].wait()
     partial = one_row_dot(activated, ada[...])
-    mods[me] = jnp.concatenate(
+    mods[me // 2] = jnp.concatenate(
         [partial[:, :width], partial[:, width : 2 * width]], axis=0
     ).astype(BF16)
     span = gates.shape[2]
-    gates[me] = jnp.concatenate(
+    gates[me // 2] = jnp.concatenate(
         [partial[:, 2 * width : 2 * width + span], partial[:, 3 * width - span :]], axis=0
     ).astype(BF16)
-    loads[4].start()
+    for load in qkv_loads:
+        load.start()
     ow_load = pltpu.make_async_copy(ow_h, ow, wsem.at[0])
     ow_load.start()
 
     pl.semaphore_wait(barrier, n - 1)
 
-    @pl.loop(1, n)
+    half_n = n // 2
+
+    @pl.loop(1, half_n)
     def _(step):
-        remote(mods.at[me], mods.at[me], msend, mrecv, lax.rem(me + step, n)).start()
+        row = me // 2
+        remote(mods.at[row], mods.at[row], msend, mrecv, lax.rem(me + 2 * step, n)).start()
 
     ids = lax.broadcasted_iota(jnp.int32, (rows, rows), 0)
     eye = ids == lax.broadcasted_iota(jnp.int32, (rows, rows), 1)
@@ -182,15 +208,26 @@
     norm = centered * lax.rsqrt(variance + 1e-6)
     norm_s[...] = norm
     nsend[...] = norm.astype(BF16)
-    mirror_copy = remote(nsend, ngot, nsem, nrecv, mirror)
-    mirror_copy.start()
-
-    drain(mods.at[pl.ds(0, n - 1)], mrecv)
-    modulation = jnp.sum(mods[...].astype(F32), axis=0)
+    norm_copies = [
+        pltpu.make_async_remote_copy(
+            src_ref=nsend, dst_ref=dst, send_sem=nsem.at[i], recv_sem=nrecv.at[i],
+            device_id={"patch": to}, device_id_type=MESH,
+        )
+        for i, (dst, to) in enumerate([(ngot, mirror), (zgot, flip(me, 4)), (xgot, flip(me, 2))])
+    ]
+    for copy in norm_copies:
+        copy.start()
+
+    drain(mods.at[pl.ds(0, half_n - 1)], mrecv)
+    partner = flip(me, 1)
+    msum[...] = jnp.sum(mods[...].astype(F32), axis=0)
+    sum_copy = remote(msum, mgot, hsend, hrecv, partner)
+    sum_copy.start()
+    sum_copy.wait_recv()
+    modulation = msum[...] + mgot[...]
     shift = modulation[0:1]
     gain = 1.0 + modulation[1:2]
     modulated = (norm_s[...] * gain + shift).astype(BF16)
-    loads[4].wait()
 
     lane_ids = lax.broadcasted_iota(jnp.int32, (rows, LANE), 1)
 
@@ -205,51 +242,99 @@
             base = jnp.where(lanes == low + 1, bias, base)
         return base
 
-    def project(first, x):
-        return [dot(x, qkv[:, i * width : (i + 1) * width]) for i in range(first, 3)]
-
-    def pack(parts, base, fold_group, stride, buffer):
+    def pack(parts, p, low, base, fold_group, stride, write):
+        cut = p * ex
+        nexts = []
+        for j, part in enumerate(parts):
+            here = part[:, low : low + LANE]
+            after = part[:, low + LANE : low + 2 * LANE]
+            nexts.append(after)
+            mixed = jnp.where(lane_ids < cut, after, here)
+            write(slice(j * rows, (j + 1) * rows), mixed.astype(BF16))
+        packed = fold(nexts, base, fold_group, stride, ex, cut)
+        write(slice(len(parts) * rows, None), packed.astype(BF16))
+
+    def into(ref, index):
+        def write(part, value):
+            ref[index, part, :] = value
+
+        return write
+
+    def pair_parts(x, weights):
+        product = dot(x, weights[...])
+        parts = [product[:, i * reach : (i + 1) * reach] for i in range(3)]
+        return [parts[0] * scale_q] + parts[1:]
+
+    my_slot = group * PAIRS + pair
+    slots = groups * PAIRS
+    block_of = me - pair
+    pltpu.make_async_copy(far_w, far_w, wsem.at[1]).wait()
+    base0 = base_of(me, fold0, stride0, 3)
+    parts = pair_parts(modulated, far_w)
+    for q in range(2):
+        pack(parts, 2 * far_chip + q, q * LANE, base0, fold0, stride0, into(sendd, q))
+    for q in range(2):
+        remote(sendd.at[q], got0.at[pair], dsend, drecv, block_of + 2 * far_chip + q).start()
+
+    pltpu.make_async_copy(kv_w, kv_w, wsem.at[3]).wait()
+
+    def kv_pack(x, owner, buffer):
+        base = base_of(owner, fold1, stride1, 2)
+        parts = [dot(x, kv_w[:, i * width : (i + 1) * width]) for i in range(2)]
         for p in range(PAIRS):
-            low, cut = p * LANE, p * ex
-            nexts = []
-            for j, part in enumerate(parts):
-                here = part[:, low : low + LANE]
-                after = part[:, low + LANE : low + 2 * LANE]
-                nexts.append(after)
-                mixed = jnp.where(lane_ids < cut, after, here) if cut else here
-                buffer[p, j * rows : (j + 1) * rows, :] = mixed.astype(BF16)
-            packed = fold(nexts, base, fold_group, stride, ex, cut)
-            buffer[p, len(parts) * rows :, :] = packed.astype(BF16)
-
-    def spread(buffer, got, send, recv):
-        slot = group * PAIRS + pair
-
-        @pl.loop(1, groups * PAIRS)
-        def _(j):
-            turn = lax.rem(slot + j, groups * PAIRS)
-            to = turn // PAIRS * HEADS + side * PAIRS + lax.rem(turn, PAIRS)
-            remote(buffer.at[lax.rem(turn, PAIRS)], got.at[slot], send, recv, to).start()
-
-        got[slot] = buffer[pair]
-
-    parts = project(0, modulated)
-    pack([parts[0] * scale_q] + parts[1:], base_of(me, fold0, stride0, 3), fold0, stride0, send0)
-    spread(send0, got0, psend, precv)
-
-    @pl.loop(1, n)
+            pack(parts, p, p * LANE, base, fold1, stride1, into(buffer, p))
+
+    def spread(buffer, got, send, recv, g):
+        for j in range(1 if g is None else 0, PAIRS):
+            turn = lax.rem(pair + j, PAIRS)
+            to = (group if g is None else g) * HEADS + side * PAIRS + turn
+            remote(buffer.at[turn], got.at[my_slot], send, recv, to).start()
+
+    if groups > 1:
+        kv_pack(modulated, me, send2)
+
+        @pl.loop(1, groups)
+        def _(g):
+            spread(send2, got2, tsend, trecv, lax.rem(group + g, groups))
+
+    norm_copies[0].wait_recv()
+    kv_pack((ngot[...].astype(F32) * gain + shift).astype(BF16), mirror, send1)
+    spread(send1, got1, rsend, rrecv, None)
+    if groups > 1:
+
+        @pl.loop(1, groups)
+        def _(g):
+            spread(send1, got1, rsend, rrecv, lax.rem(group + g, groups))
+
+    got1[my_slot] = send1[pair]
+
+    @pl.loop(1, half_n)
     def _(step):
-        remote(gates.at[me], gates.at[me], gsend, grecv, lax.rem(me + step, n)).start()
-
-    mirror_copy.wait_recv()
-    modulated = (ngot[...].astype(F32) * gain + shift).astype(BF16)
-    pack(project(1, modulated), base_of(mirror, fold1, stride1, 2), fold1, stride1, send1)
-    spread(send1, got1, rsend, rrecv)
-
-    slots = groups * PAIRS
-    drain(got0.at[pl.ds(0, slots - 1)], precv)
+        row = me // 2
+        remote(gates.at[row], gates.at[row], gsend, grecv, lax.rem(me + 2 * step, n)).start()
+
+    pltpu.make_async_copy(near_w, near_w, wsem.at[2]).wait()
+    norm_copies[1].wait_recv()
+    norm_copies[2].wait_recv()
+    others = [(ref[...].astype(F32) * gain + shift).astype(BF16) for ref in (xgot, zgot)]
+    parts = pair_parts(jnp.concatenate([modulated] + others, axis=0), near_w)
+    owners = [pair, flip(pair, 2), flip(pair, 4)]
+    bases = [base0] + [base_of(block_of + owner, fold0, stride0, 3) for owner in owners[1:]]
+    mine = lax.rem(pair, 2)
+    for b in range(3):
+        own = [part[b * rows : (b + 1) * rows] for part in parts]
+        for q in range(2):
+            pack(own, 2 * chip + q, q * LANE, bases[b], fold0, stride0, into(sendp, 2 * b + q))
+    for b in range(3):
+        remote(sendp.at[2 * b + 1 - mine], got0.at[owners[b]], psend, precv, partner).start()
+    for b in range(3):
+        got0[owners[b]] = sendp[2 * b + mine]
+
+    drain(got0.at[pl.ds(0, 3)], precv)
+    drain(got0.at[pl.ds(0, 2)], drecv)
 
     def keys_of(got, g, first, fold_group, stride, to):
-        block = got[g * PAIRS : (g + 1) * PAIRS]
+        block = got[pl.ds(g * PAIRS, PAIRS)]
         cells = PAIRS * rows
         k = block[:, first * rows : (first + 1) * rows].reshape(cells, LANE)
         v = block[:, (first + 1) * rows : (first + 2) * rows].reshape(cells, LANE)
@@ -268,7 +353,7 @@
     bias_one = jnp.where(q_lanes == 3 * ex + 1, 1.0, 0.0)
 
     def queries_of(base):
-        block = got0[pl.ds(group * PAIRS + base, half)]
+        block = got0[pl.ds(base, half)]
         qa = block[:, :rows].reshape(cells, LANE).astype(F32)
         extra = jnp.concatenate(
             [
@@ -282,8 +367,8 @@
         low = jnp.concatenate([jnp.where(first_head, 0.0, qa), extra], axis=1)
         return jnp.concatenate([top, low], axis=0).astype(BF16)
 
-    bases = [(1 - near) * half, near * half]
-    queries = [queries_of(base) for base in bases]
+    starts = [(1 - near) * half, near * half]
+    queries = [queries_of(base) for base in starts]
 
     def attend(i, keys, values, first):
         scores = dot_t(queries[i], keys)
@@ -301,18 +386,21 @@
         top_s[i] = jnp.broadcast_to(state[0], top_s.shape[1:])
         o_s[i] = state[1]
 
-    for g in range(groups):
-        keys, values = keys_of(got0, g, 1, fold0, stride0, 0)
-        for i in range(2):
-            keep(i, attend(i, keys, values, g == 0))
-
+    keys, values = keys_of(got0, 0, 1, fold0, stride0, 0)
+    for i in range(2):
+        keep(i, attend(i, keys, values, True))
+
+    if groups > 1:
+        drain(got2.at[pl.ds(0, slots - PAIRS)], trecv)
     drain(got1.at[pl.ds(0, slots - 1)], rrecv)
-    for g in range(groups - 1):
-        keys, values = keys_of(got1, g, 0, fold1, stride1, ex)
-        for i in range(2):
-            keep(i, attend(i, keys, values, False))
-
-    keys, values = keys_of(got1, groups - 1, 0, fold1, stride1, ex)
+    for g in range(1, groups):
+        other = lax.rem(group + g, groups)
+        for got in (got1, got2):
+            keys, values = keys_of(got, other, 0, fold1, stride1, ex)
+            for i in range(2):
+                keep(i, attend(i, keys, values, False))
+
+    keys, values = keys_of(got1, group, 0, fold1, stride1, ex)
     fold_zero = jnp.zeros((fold2, LANE), F32)
     for i in range(2):
         _, mixed = attend(i, keys, values, False)
@@ -322,34 +410,38 @@
         extra = mixed[cells:, LANE:]
         for s in range(half):
             span_s = slice(s * rows, (s + 1) * rows)
-            slot = bases[i] + s
+            slot = starts[i] + s
             att[slot, :rows, :] = main[span_s].astype(BF16)
             att[slot, rows:, :] = fold(
                 [extra[span_s]], fold_zero, fold2, ex, ex, 2 * ex
             ).astype(BF16)
-        for s in range(half):
-            slot = bases[i] + s
-
-            @pl.when(slot != pair)
-            def _():
-                remote(
-                    att.at[slot], back.at[pair], asend, arecv, me - pair + slot
-                ).start()
-
+        for s in range(i, half):
+            slot = starts[i] + lax.rem(pair + s, half)
+            remote(att.at[slot], back.at[pair], asend, arecv, me - pair + slot).start()
+
+    drain(gates.at[pl.ds(0, half_n - 1)], grecv)
+    gsum[...] = jnp.sum(gates[...].astype(F32), axis=0)
+    gate_copy = remote(gsum, ggot, fsend, frecv, partner)
+    gate_copy.start()
     back[pair] = att[pair]
     ow_load.wait()
-    drain(gates.at[pl.ds(0, n - 1)], grecv)
-    gate_rows = jnp.sum(gates[...].astype(F32), axis=0)
-    gate = jnp.concatenate([gate_rows[0:1], gate_rows[1:2, 2 * span - width :]], axis=1)
     valid = (lax.broadcasted_iota(jnp.int32, (rows, 1), 0) < counts[me]).astype(F32)
 
-    drain(mods.at[pl.ds(0, n - 1)], msend)
-    drain(gates.at[pl.ds(0, n - 1)], gsend)
-    mirror_copy.wait_send()
-    drain(got0.at[pl.ds(0, slots - 1)], psend)
+    drain(mods.at[pl.ds(0, half_n - 1)], msend)
+    drain(gates.at[pl.ds(0, half_n - 1)], gsend)
+    sum_copy.wait_send()
+    for copy in norm_copies:
+        copy.wait_send()
+    drain(got0.at[pl.ds(0, 2)], dsend)
+    drain(got0.at[pl.ds(0, 3)], psend)
+    if groups > 1:
+        drain(got2.at[pl.ds(0, slots - PAIRS)], tsend)
     drain(got1.at[pl.ds(0, slots - 1)], rsend)
     drain(back.at[pl.ds(0, PAIRS - 1)], arecv)
 
+    gate_copy.wait()
+    gate_rows = gsum[...] + ggot[...]
+    gate = jnp.concatenate([gate_rows[0:1], gate_rows[1:2, 2 * span - width :]], axis=1)
     rest = jnp.zeros((rows, LANE), F32)
     for p in range(PAIRS):
         piece = unfold(back[p, rows:, :].astype(F32), rows, ex, p * ex)
@@ -390,6 +482,7 @@
     size2 = rows + fold_rows(rows, ex)
     slots = n // 2
     queries = PAIRS * rows
+    span = -(-width // 256) * LANE
     pos_tab, time_tab = tables(width, time_in.shape[0])
     hbm = pl.BlockSpec(memory_space=pl.ANY)
     vmem = pl.BlockSpec(memory_space=pltpu.VMEM)
@@ -409,17 +502,28 @@
             pltpu.VMEM(time_in.shape, BF16),
             pltpu.VMEM(time_out.shape[::-1], BF16),
             pltpu.VMEM(ada_weight.shape, BF16),
-            pltpu.VMEM(qkv_weight.shape, BF16),
+            pltpu.VMEM((width, 9 * LANE), BF16),
+            pltpu.VMEM((width, 9 * LANE), BF16),
+            pltpu.VMEM((width, 2 * width), BF16),
             pltpu.VMEM(out_weight.shape, BF16),
-            pltpu.VMEM((n, 2, width), BF16),
-            pltpu.VMEM((n, 2, -(-width // 256) * 128), BF16),
+            pltpu.VMEM((n // 2, 2, width), BF16),
+            pltpu.VMEM((n // 2, 2, span), BF16),
+            pltpu.VMEM((2, width), F32),
+            pltpu.VMEM((2, width), F32),
+            pltpu.VMEM((2, span), F32),
+            pltpu.VMEM((2, span), F32),
             pltpu.VMEM((rows, width), F32),
             pltpu.VMEM((rows, width), F32),
             pltpu.VMEM((rows, width), BF16),
             pltpu.VMEM((rows, width), BF16),
+            pltpu.VMEM((rows, width), BF16),
+            pltpu.VMEM((rows, width), BF16),
+            pltpu.VMEM((2, size0, LANE), BF16),
+            pltpu.VMEM((6, size0, LANE), BF16),
+            pltpu.VMEM((PAIRS, size1, LANE), BF16),
+            pltpu.VMEM((PAIRS, size1, LANE), BF16),
             pltpu.VMEM((PAIRS, size0, LANE), BF16),
-            pltpu.VMEM((PAIRS, size1, LANE), BF16),
-            pltpu.VMEM((slots, size0, LANE), BF16),
+            pltpu.VMEM((slots, size1, LANE), BF16),
             pltpu.VMEM((slots, size1, LANE), BF16),
             pltpu.VMEM((2, queries, 2 * LANE), F32),
             pltpu.VMEM((2, queries, LANE), F32),
@@ -428,7 +532,7 @@
             dma((5,)),
             dma((5,)),
         ]
-        + [dma((1,))] * 13,
+        + [dma((4,))] + [dma((1,))] * 4 + [dma((3,))] * 2 + [dma((1,))] * 14,
         compiler_params=pltpu.CompilerParams(
             collective_id=0, has_side_effects=True, vmem_limit_bytes=60 * 2**20
         ),

time: 28.4 us -> 26.4 us (0.930)
  Pallas kernels: 27 us -> 25 us
    pallas_call x1, Pallas kernels: 27 us -> 25 us  [per_device(): pl.pallas_call(functools.partial(block_kernel, n, rows, width, head), out...]
where the time goes in v3:
time: 26.4 us; the launch traced here: 26.3 us
  Pallas kernels  25 us (95%)
  between operations  0.66 us (2%)
  local copies, waits for them, and re-layouts  0.65 us (2%)
    pallas_call x1, Pallas kernels, per_device(): pl.pallas_call(functools.partial(block_kernel, n, rows, width, head), out...  25 us
    unnamed x1, local copies, waits for them, and re-layouts  0.65 us

profile of v3, /device:TPU:0, one launch (start us, length us, event | category | flops | bytes accessed | tf_op | source)
XLA Modules:
  0.0 26.3 jit_solution(13813899135069245211)
XLA Ops:
  0.7 25.0 %shard_map.109 = bf16[48,1152]{1,0:T(8,128)(2,1)S(1)} custom-call(s32[16]{0:T(128)} %counts_h.1, s32[1]{0:T(128)S(6)} %copy.14.tstep_h, s32[2,48]{1,0:T(2,128)} %pos_h.1, f32[2,1152]{1,0:T(2,128)} %constant.4.clone.pos_tab_h, f32[2,256]{1,0:T(2,128)} %constant.5.clone.time_tab_h, bf16[48,1152]{1,0:T(8,128)(2,1)} %tok_h.1, bf16[256,1152]{1,0:T(8,128)(2,1)} %tin_h.1, ...), custom_call_target="tpu_custom_call" | custom-call | tf_op jit(solution)/shard_map/pallas_call | solution.py:490
  25.6 0.6 %copy.13 = bf16[48,1152]{1,0:T(8,128)(2,1)} copy(bf16[48,1152]{1,0:T(8,128)(2,1)S(1)} %shard_map.109) | data formatting | bytes 221184

commit v4 on v3

--- a/solution.py
+++ b/solution.py
@@ -94,7 +94,7 @@
     out,
     counts, tstep, pos, pos_tab, time_tab, tok, tin, tout, ada, near_w, far_w, kv_w, ow,
     mods, gates, msum, mgot, gsum, ggot, xin_s, norm_s, nsend, ngot, xgot, zgot, sendd, sendp, send1, send2,
-    got0, got1, got2, o_s, top_s, att, back,
+    got0, got1, got2, o_s, top_s, total_s, att, back,
     lsem, ssem, wsem, msend, mrecv, gsend, grecv, nsem, nrecv, dsend, drecv, psend, precv,
     rsend, rrecv, tsend, trecv, asend, arecv, hsend, hrecv, fsend, frecv,
 ):
@@ -103,7 +103,7 @@
     side = lax.rem(me // PAIRS, 2)
     group = me // HEADS
     groups = n // HEADS
-    mirror = me + PAIRS * (1 - 2 * side)
+    mirror = flip(flip(me, PAIRS), PAIRS // 2)
     ex = 2 * head - LANE
     stride0, stride1 = 3 * ex + 2, 2 * ex + 2
     fold0, fold1, fold2 = fold_rows(rows, stride0), fold_rows(rows, stride1), fold_rows(rows, ex)
@@ -154,11 +154,29 @@
              (pos_h, pos), (pos_tab_h, pos_tab)]
         )
     ]
-    for load in small[:2] + loads[:4] + small[2:]:
+    for load in small[2:] + loads[3:] + small[:2] + loads[:3]:
         load.start()
+
+    ids = lax.broadcasted_iota(jnp.int32, (rows, rows), 0)
+    eye = ids == lax.broadcasted_iota(jnp.int32, (rows, rows), 1)
+    for load in small[2:]:
+        load.wait()
+    posf = pos[...].astype(F32)
+    row_col = jnp.sum(jnp.where(eye, posf[0:1, :], 0.0), axis=1, keepdims=True)
+    col_col = jnp.sum(jnp.where(eye, posf[1:2, :], 0.0), axis=1, keepdims=True)
+    wide_lanes = lax.broadcasted_iota(jnp.int32, (1, width), 1)
+    place = jnp.where(wide_lanes < width // 2, row_col, col_col)
+    embed = sine(place * pos_tab[0:1, :] + pos_tab[1:2, :])
+    loads[3].wait()
+    x_in = tok[...].astype(F32) + embed
+    xin_s[...] = x_in
+    centered = x_in - jnp.mean(x_in, axis=1, keepdims=True)
+    variance = jnp.mean(centered * centered, axis=1, keepdims=True)
+    norm = centered * lax.rsqrt(variance + 1e-6)
+    norm_s[...] = norm
+    nsend[...] = norm.astype(BF16)
     for load in small[:2]:
         load.wait()
-
     angles = tstep[0].astype(F32) * time_tab[0:1, :] + time_tab[1:2, :]
     features = sine(angles).astype(BF16)
     loads[0].wait()
@@ -190,24 +208,6 @@
         row = me // 2
         remote(mods.at[row], mods.at[row], msend, mrecv, lax.rem(me + 2 * step, n)).start()
 
-    ids = lax.broadcasted_iota(jnp.int32, (rows, rows), 0)
-    eye = ids == lax.broadcasted_iota(jnp.int32, (rows, rows), 1)
-    for load in small[2:]:
-        load.wait()
-    posf = pos[...].astype(F32)
-    row_col = jnp.sum(jnp.where(eye, posf[0:1, :], 0.0), axis=1, keepdims=True)
-    col_col = jnp.sum(jnp.where(eye, posf[1:2, :], 0.0), axis=1, keepdims=True)
-    wide_lanes = lax.broadcasted_iota(jnp.int32, (1, width), 1)
-    place = jnp.where(wide_lanes < width // 2, row_col, col_col)
-    embed = sine(place * pos_tab[0:1, :] + pos_tab[1:2, :])
-    loads[3].wait()
-    x_in = tok[...].astype(F32) + embed
-    xin_s[...] = x_in
-    centered = x_in - jnp.mean(x_in, axis=1, keepdims=True)
-    variance = jnp.mean(centered * centered, axis=1, keepdims=True)
-    norm = centered * lax.rsqrt(variance + 1e-6)
-    norm_s[...] = norm
-    nsend[...] = norm.astype(BF16)
     norm_copies = [
         pltpu.make_async_remote_copy(
             src_ref=nsend, dst_ref=dst, send_sem=nsem.at[i], recv_sem=nrecv.at[i],
@@ -342,7 +342,13 @@
             [unfold(block[s, (first + 2) * rows :].astype(F32), rows, stride, to) for s in range(PAIRS)],
             axis=0,
         ).astype(BF16)
-        return jnp.concatenate([k, extra], axis=1), jnp.concatenate([v, extra], axis=1)
+        lanes = lax.broadcasted_iota(jnp.int32, (cells, LANE), 1)
+        copies = jnp.where(lanes < ex, pltpu.roll(extra, LANE - 2 * ex, axis=1), 0.0).astype(BF16)
+        step = ex
+        while step < LANE:
+            copies = copies + pltpu.roll(copies, step, axis=1)
+            step *= 2
+        return jnp.concatenate([k, extra], axis=1), jnp.concatenate([v, copies], axis=1)
 
     half = PAIRS // 2
     cells = half * rows
@@ -370,21 +376,27 @@
     starts = [(1 - near) * half, near * half]
     queries = [queries_of(base) for base in starts]
 
+    def wide(x, count):
+        return jnp.concatenate([x] * count, axis=1)
+
     def attend(i, keys, values, first):
         scores = dot_t(queries[i], keys)
-        top = jnp.max(scores, axis=1, keepdims=True)
+        shape = (scores.shape[0], LANE)
+        top = jnp.broadcast_to(jnp.max(scores, axis=1, keepdims=True), shape)
         if not first:
-            before = top_s[i][:, 0:1]
+            before = top_s[i]
             top = jnp.maximum(top, before)
-        prob = jnp.exp2(scores - top).astype(BF16)
-        mixed = dot(prob, values)
+        prob = jnp.exp2(scores - wide(top, scores.shape[1] // LANE))
+        total = jnp.broadcast_to(jnp.sum(prob, axis=1, keepdims=True), shape)
+        mixed = dot(prob.astype(BF16), values)
         if not first:
-            mixed = o_s[i] * jnp.exp2(before - top) + mixed
-        return top, mixed
+            decay = jnp.exp2(before - top)
+            total = total_s[i] * decay + total
+            mixed = o_s[i] * wide(decay, 2) + mixed
+        return top, total, mixed
 
     def keep(i, state):
-        top_s[i] = jnp.broadcast_to(state[0], top_s.shape[1:])
-        o_s[i] = state[1]
+        top_s[i], total_s[i], o_s[i] = state
 
     keys, values = keys_of(got0, 0, 1, fold0, stride0, 0)
     for i in range(2):
@@ -402,19 +414,23 @@
 
     keys, values = keys_of(got1, group, 0, fold1, stride1, ex)
     fold_zero = jnp.zeros((fold2, LANE), F32)
+    fold_lanes = lax.broadcasted_iota(jnp.int32, (fold2, LANE), 1)
     for i in range(2):
-        _, mixed = attend(i, keys, values, False)
-        share = 1.0 / mixed[:, LANE + 3 * ex : LANE + 3 * ex + 1]
-        mixed = mixed * share
+        _, total, mixed = attend(i, keys, values, False)
+        mixed = mixed * wide(1.0 / total, 2)
         main = jnp.where(first_head, mixed[:cells, :LANE], mixed[cells:, :LANE])
         extra = mixed[cells:, LANE:]
         for s in range(half):
             span_s = slice(s * rows, (s + 1) * rows)
             slot = starts[i] + s
             att[slot, :rows, :] = main[span_s].astype(BF16)
-            att[slot, rows:, :] = fold(
-                [extra[span_s]], fold_zero, fold2, ex, ex, 2 * ex
-            ).astype(BF16)
+            packed = fold_zero
+            for r in range(rows // fold2):
+                low = s * rows + r * fold2
+                packed = jnp.where(
+                    (fold_lanes >= r * ex) & (fold_lanes < (r + 1) * ex), extra[low : low + fold2], packed
+                )
+            att[slot, rows:, :] = packed.astype(BF16)
         for s in range(i, half):
             slot = starts[i] + lax.rem(pair + s, half)
             remote(att.at[slot], back.at[pair], asend, arecv, me - pair + slot).start()
@@ -527,6 +543,7 @@
             pltpu.VMEM((slots, size1, LANE), BF16),
             pltpu.VMEM((2, queries, 2 * LANE), F32),
             pltpu.VMEM((2, queries, LANE), F32),
+            pltpu.VMEM((2, queries, LANE), F32),
             pltpu.VMEM((PAIRS, size2, LANE), BF16),
             pltpu.VMEM((PAIRS, size2, LANE), BF16),
             dma((5,)),

time: 26.4 us -> 25.6 us (0.970)
  Pallas kernels: 25 us -> 24.2 us
    pallas_call x1, Pallas kernels: 25 us -> 24.2 us  [per_device(): pl.pallas_call(functools.partial(block_kernel, n, rows, width, head), out...]
where the time goes in v4:
time: 25.6 us; the launch traced here: 25.5 us
  Pallas kernels  24.2 us (95%)
  between operations  0.66 us (3%)
  local copies, waits for them, and re-layouts  0.65 us (3%)
    pallas_call x1, Pallas kernels, per_device(): pl.pallas_call(functools.partial(block_kernel, n, rows, width, head), out...  24.2 us
    unnamed x1, local copies, waits for them, and re-layouts  0.65 us

profile of v4, /device:TPU:0, one launch (start us, length us, event | category | flops | bytes accessed | tf_op | source)
XLA Modules:
  0.0 25.5 jit_solution(2791800427096142476)
XLA Ops:
  0.7 24.2 %shard_map.109 = bf16[48,1152]{1,0:T(8,128)(2,1)S(1)} custom-call(s32[16]{0:T(128)} %counts_h.1, s32[1]{0:T(128)S(6)} %copy.14.tstep_h, s32[2,48]{1,0:T(2,128)} %pos_h.1, f32[2,1152]{1,0:T(2,128)} %constant.4.clone.pos_tab_h, f32[2,256]{1,0:T(2,128)} %constant.5.clone.time_tab_h, bf16[48,1152]{1,0:T(8,128)(2,1)} %tok_h.1, bf16[256,1152]{1,0:T(8,128)(2,1)} %tin_h.1, ...), custom_call_target="tpu_custom_call" | custom-call | tf_op jit(solution)/shard_map/pallas_call | solution.py:506
  24.8 0.6 %copy.13 = bf16[48,1152]{1,0:T(8,128)(2,1)} copy(bf16[48,1152]{1,0:T(8,128)(2,1)S(1)} %shard_map.109) | data formatting | bytes 221184

commit v5 on v4

--- a/solution.py
+++ b/solution.py
@@ -93,7 +93,7 @@
     tok_h, tin_h, tout_h, ada_h, qkv_h, ow_h,
     out,
     counts, tstep, pos, pos_tab, time_tab, tok, tin, tout, ada, near_w, far_w, kv_w, ow,
-    mods, gates, msum, mgot, gsum, ggot, xin_s, norm_s, nsend, ngot, xgot, zgot, sendd, sendp, send1, send2,
+    mods, gates, msum, gsum, xin_s, norm_s, nsend, ngot, xgot, zgot, sendd, sendp, send1, send2,
     got0, got1, got2, o_s, top_s, total_s, att, back,
     lsem, ssem, wsem, msend, mrecv, gsend, grecv, nsem, nrecv, dsend, drecv, psend, precv,
     rsend, rrecv, tsend, trecv, asend, arecv, hsend, hrecv, fsend, frecv,
@@ -187,11 +187,11 @@
     activated = silu(cond[0:1]).astype(BF16)
     loads[2].wait()
     partial = one_row_dot(activated, ada[...])
-    mods[me // 2] = jnp.concatenate(
+    mods[me] = jnp.concatenate(
         [partial[:, :width], partial[:, width : 2 * width]], axis=0
     ).astype(BF16)
     span = gates.shape[2]
-    gates[me // 2] = jnp.concatenate(
+    gates[me] = jnp.concatenate(
         [partial[:, 2 * width : 2 * width + span], partial[:, 3 * width - span :]], axis=0
     ).astype(BF16)
     for load in qkv_loads:
@@ -201,12 +201,37 @@
 
     pl.semaphore_wait(barrier, n - 1)
 
+    core = lax.rem(me, 2)
+    partner = flip(me, 1)
     half_n = n // 2
 
-    @pl.loop(1, half_n)
-    def _(step):
-        row = me // 2
-        remote(mods.at[row], mods.at[row], msend, mrecv, lax.rem(me + 2 * step, n)).start()
+    def to_odd(ref, send, recv):
+        @pl.loop(1, half_n)
+        def _(step):
+            to = 2 * lax.rem(me // 2 + step, half_n) + 1
+            remote(ref.at[me], ref.at[me], send, recv, to).start()
+
+        @pl.when(core == 0)
+        def _():
+            remote(ref.at[me], ref.at[me], send, recv, partner).start()
+
+    def total_of(ref, total, recv, send, done):
+        @pl.when(core == 1)
+        def _():
+            drain(ref.at[pl.ds(0, n - 1)], recv)
+            total[...] = jnp.sum(ref[...].astype(F32), axis=0)
+            remote(total, total, send, done, partner).start()
+
+    def sent(ref, send):
+        @pl.when(core == 0)
+        def _():
+            drain(ref.at[pl.ds(0, half_n)], send)
+
+        @pl.when(core == 1)
+        def _():
+            drain(ref.at[pl.ds(0, half_n - 1)], send)
+
+    to_odd(mods, msend, mrecv)
 
     norm_copies = [
         pltpu.make_async_remote_copy(
@@ -218,13 +243,13 @@
     for copy in norm_copies:
         copy.start()
 
-    drain(mods.at[pl.ds(0, half_n - 1)], mrecv)
-    partner = flip(me, 1)
-    msum[...] = jnp.sum(mods[...].astype(F32), axis=0)
-    sum_copy = remote(msum, mgot, hsend, hrecv, partner)
-    sum_copy.start()
-    sum_copy.wait_recv()
-    modulation = msum[...] + mgot[...]
+    total_of(mods, msum, mrecv, hsend, hrecv)
+
+    @pl.when(core == 0)
+    def _():
+        drain(msum, hrecv)
+
+    modulation = msum[...]
     shift = modulation[0:1]
     gain = 1.0 + modulation[1:2]
     modulated = (norm_s[...] * gain + shift).astype(BF16)
@@ -308,10 +333,7 @@
 
     got1[my_slot] = send1[pair]
 
-    @pl.loop(1, half_n)
-    def _(step):
-        row = me // 2
-        remote(gates.at[row], gates.at[row], gsend, grecv, lax.rem(me + 2 * step, n)).start()
+    to_odd(gates, gsend, grecv)
 
     pltpu.make_async_copy(near_w, near_w, wsem.at[2]).wait()
     norm_copies[1].wait_recv()
@@ -435,17 +457,18 @@
             slot = starts[i] + lax.rem(pair + s, half)
             remote(att.at[slot], back.at[pair], asend, arecv, me - pair + slot).start()
 
-    drain(gates.at[pl.ds(0, half_n - 1)], grecv)
-    gsum[...] = jnp.sum(gates[...].astype(F32), axis=0)
-    gate_copy = remote(gsum, ggot, fsend, frecv, partner)
-    gate_copy.start()
+    total_of(gates, gsum, grecv, fsend, frecv)
     back[pair] = att[pair]
     ow_load.wait()
     valid = (lax.broadcasted_iota(jnp.int32, (rows, 1), 0) < counts[me]).astype(F32)
 
-    drain(mods.at[pl.ds(0, half_n - 1)], msend)
-    drain(gates.at[pl.ds(0, half_n - 1)], gsend)
-    sum_copy.wait_send()
+    sent(mods, msend)
+    sent(gates, gsend)
+
+    @pl.when(core == 1)
+    def _():
+        drain(msum, hsend)
+
     for copy in norm_copies:
         copy.wait_send()
     drain(got0.at[pl.ds(0, 2)], dsend)
@@ -455,8 +478,16 @@
     drain(got1.at[pl.ds(0, slots - 1)], rsend)
     drain(back.at[pl.ds(0, PAIRS - 1)], arecv)
 
-    gate_copy.wait()
-    gate_rows = gsum[...] + ggot[...]
+
+    @pl.when(core == 1)
+    def _():
+        drain(gsum, fsend)
+
+    @pl.when(core == 0)
+    def _():
+        drain(gsum, frecv)
+
+    gate_rows = gsum[...]
     gate = jnp.concatenate([gate_rows[0:1], gate_rows[1:2, 2 * span - width :]], axis=1)
     rest = jnp.zeros((rows, LANE), F32)
     for p in range(PAIRS):
@@ -522,11 +553,9 @@
             pltpu.VMEM((width, 9 * LANE), BF16),
             pltpu.VMEM((width, 2 * width), BF16),
             pltpu.VMEM(out_weight.shape, BF16),
-            pltpu.VMEM((n // 2, 2, width), BF16),
-            pltpu.VMEM((n // 2, 2, span), BF16),
+            pltpu.VMEM((n, 2, width), BF16),
+            pltpu.VMEM((n, 2, span), BF16),
             pltpu.VMEM((2, width), F32),
-            pltpu.VMEM((2, width), F32),
-            pltpu.VMEM((2, span), F32),
             pltpu.VMEM((2, span), F32),
             pltpu.VMEM((rows, width), F32),
             pltpu.VMEM((rows, width), F32),

time: 25.6 us -> 25 us (0.977)
  Pallas kernels: 24.2 us -> 23.6 us
    pallas_call x1, Pallas kernels: 24.2 us -> 23.6 us  [per_device(): pl.pallas_call(functools.partial(block_kernel, n, rows, width, head), out...]
where the time goes in v5:
time: 25 us; the launch traced here: 24.9 us
  Pallas kernels  23.6 us (94%)
  between operations  0.66 us (3%)
  local copies, waits for them, and re-layouts  0.65 us (3%)
    pallas_call x1, Pallas kernels, per_device(): pl.pallas_call(functools.partial(block_kernel, n, rows, width, head), out...  23.6 us
    unnamed x1, local copies, waits for them, and re-layouts  0.65 us

profile of v5, /device:TPU:0, one launch (start us, length us, event | category | flops | bytes accessed | tf_op | source)
XLA Modules:
  0.0 24.9 jit_solution(10996652134179062965)
XLA Ops:
  0.7 23.6 %shard_map.109 = bf16[48,1152]{1,0:T(8,128)(2,1)S(1)} custom-call(s32[16]{0:T(128)} %counts_h.1, s32[1]{0:T(128)S(6)} %copy.14.tstep_h, s32[2,48]{1,0:T(2,128)} %pos_h.1, f32[2,1152]{1,0:T(2,128)} %constant.4.clone.pos_tab_h, f32[2,256]{1,0:T(2,128)} %constant.5.clone.time_tab_h, bf16[48,1152]{1,0:T(8,128)(2,1)} %tok_h.1, bf16[256,1152]{1,0:T(8,128)(2,1)} %tin_h.1, ...), custom_call_target="tpu_custom_call" | custom-call | tf_op jit(solution)/shard_map/pallas_call | solution.py:537
  24.2 0.6 %copy.13 = bf16[48,1152]{1,0:T(8,128)(2,1)} copy(bf16[48,1152]{1,0:T(8,128)(2,1)S(1)} %shard_map.109) | data formatting | bytes 221184

commit v6 on v5

--- a/solution.py
+++ b/solution.py
@@ -120,11 +120,8 @@
             device_id={"patch": to}, device_id_type=MESH,
         )
 
-    @pl.loop(1, n)
-    def _(step):
-        pl.semaphore_signal(
-            barrier, inc=1, device_id={"patch": lax.rem(me + step, n)}, device_id_type=MESH
-        )
+    def greet(to):
+        pl.semaphore_signal(barrier, inc=1, device_id={"patch": to}, device_id_type=MESH)
 
     loads = [
         pltpu.make_async_copy(src, dst, lsem.at[i])
@@ -156,6 +153,22 @@
     ]
     for load in small[2:] + loads[3:] + small[:2] + loads[:3]:
         load.start()
+
+    @pl.when(lax.rem(me, 2) == 1)
+    def _():
+        @pl.loop(1, n)
+        def _(step):
+            greet(lax.rem(me + step, n))
+
+    @pl.when(lax.rem(me, 2) == 0)
+    def _():
+        greet(mirror)
+
+        @pl.loop(1, n // 2)
+        def _(step):
+            turn = lax.rem(me // HEADS * PAIRS + pair + step, n // 2)
+            greet(turn // PAIRS * HEADS + side * PAIRS + lax.rem(turn, PAIRS))
+
 
     ids = lax.broadcasted_iota(jnp.int32, (rows, rows), 0)
     eye = ids == lax.broadcasted_iota(jnp.int32, (rows, rows), 1)
@@ -199,7 +212,15 @@
     ow_load = pltpu.make_async_copy(ow_h, ow, wsem.at[0])
     ow_load.start()
 
-    pl.semaphore_wait(barrier, n - 1)
+
+    @pl.when(lax.rem(me, 2) == 1)
+    def _():
+        pl.semaphore_wait(barrier, n // 4 * 3 - 1)
+
+    @pl.when(lax.rem(me, 2) == 0)
+    def _():
+        pl.semaphore_wait(barrier, n // 4 * 3)
+
 
     core = lax.rem(me, 2)
     partner = flip(me, 1)
@@ -310,8 +331,11 @@
             pack(parts, p, p * LANE, base, fold1, stride1, into(buffer, p))
 
     def spread(buffer, got, send, recv, g):
-        for j in range(1 if g is None else 0, PAIRS):
-            turn = lax.rem(pair + j, PAIRS)
+        for j in (2, 3, 6, 7, 4, 5, 1) if g is None else range(PAIRS):
+            turn = pair
+            for bit in (1, 2, 4):
+                if j & bit:
+                    turn = flip(turn, bit)
             to = (group if g is None else g) * HEADS + side * PAIRS + turn
             remote(buffer.at[turn], got.at[my_slot], send, recv, to).start()
 
@@ -437,9 +461,20 @@
     keys, values = keys_of(got1, group, 0, fold1, stride1, ex)
     fold_zero = jnp.zeros((fold2, LANE), F32)
     fold_lanes = lax.broadcasted_iota(jnp.int32, (fold2, LANE), 1)
+    scores = [dot_t(query, keys) for query in queries]
+    finals = []
     for i in range(2):
-        _, total, mixed = attend(i, keys, values, False)
-        mixed = mixed * wide(1.0 / total, 2)
+        shape = (scores[i].shape[0], LANE)
+        top = jnp.broadcast_to(jnp.max(scores[i], axis=1, keepdims=True), shape)
+        top = jnp.maximum(top, top_s[i])
+        prob = jnp.exp2(scores[i] - wide(top, scores[i].shape[1] // LANE))
+        total = jnp.broadcast_to(jnp.sum(prob, axis=1, keepdims=True), shape)
+        decay = jnp.exp2(top_s[i] - top)
+        share = 1.0 / (total_s[i] * decay + total)
+        finals.append((prob.astype(BF16), decay * share, share))
+    for i in range(2):
+        prob, old, new = finals[i]
+        mixed = o_s[i] * wide(old, 2) + dot(prob, values) * wide(new, 2)
         main = jnp.where(first_head, mixed[:cells, :LANE], mixed[cells:, :LANE])
         extra = mixed[cells:, LANE:]
         for s in range(half):
@@ -453,8 +488,11 @@
                     (fold_lanes >= r * ex) & (fold_lanes < (r + 1) * ex), extra[low : low + fold2], packed
                 )
             att[slot, rows:, :] = packed.astype(BF16)
-        for s in range(i, half):
-            slot = starts[i] + lax.rem(pair + s, half)
+        for j in (6, 7, 4, 5) if i == 0 else (2, 3, 1):
+            slot = pair
+            for bit in (1, 2, 4):
+                if j & bit:
+                    slot = flip(slot, bit)
             remote(att.at[slot], back.at[pair], asend, arecv, me - pair + slot).start()
 
     total_of(gates, gsum, grecv, fsend, frecv)

time: 25 us -> 24.5 us (0.980)
  Pallas kernels: 23.6 us -> 23 us
    pallas_call x1, Pallas kernels: 23.6 us -> 23 us  [per_device(): pl.pallas_call(functools.partial(block_kernel, n, rows, width, head), out...]
where the time goes in v6:
time: 24.5 us; the launch traced here: 24.3 us
  Pallas kernels  23 us (94%)
  between operations  0.66 us (3%)
  local copies, waits for them, and re-layouts  0.65 us (3%)
    pallas_call x1, Pallas kernels, per_device(): pl.pallas_call(functools.partial(block_kernel, n, rows, width, head), out...  23 us
    unnamed x1, local copies, waits for them, and re-layouts  0.65 us

profile of v6, /device:TPU:0, one launch (start us, length us, event | category | flops | bytes accessed | tf_op | source)
XLA Modules:
  0.0 24.3 jit_solution(3469033759188056478)
XLA Ops:
  0.7 23.0 %shard_map.109 = bf16[48,1152]{1,0:T(8,128)(2,1)S(1)} custom-call(s32[16]{0:T(128)} %counts_h.1, s32[1]{0:T(128)S(6)} %copy.14.tstep_h, s32[2,48]{1,0:T(2,128)} %pos_h.1, f32[2,1152]{1,0:T(2,128)} %constant.4.clone.pos_tab_h, f32[2,256]{1,0:T(2,128)} %constant.5.clone.time_tab_h, bf16[48,1152]{1,0:T(8,128)(2,1)} %tok_h.1, bf16[256,1152]{1,0:T(8,128)(2,1)} %tin_h.1, ...), custom_call_target="tpu_custom_call" | custom-call | tf_op jit(solution)/shard_map/pallas_call | solution.py:575
  23.6 0.6 %copy.13 = bf16[48,1152]{1,0:T(8,128)(2,1)} copy(bf16[48,1152]{1,0:T(8,128)(2,1)S(1)} %shard_map.109) | data formatting | bytes 221184

commit v7 on v6

--- a/solution.py
+++ b/solution.py
@@ -357,7 +357,6 @@
 
     got1[my_slot] = send1[pair]
 
-    to_odd(gates, gsend, grecv)
 
     pltpu.make_async_copy(near_w, near_w, wsem.at[2]).wait()
     norm_copies[1].wait_recv()
@@ -376,6 +375,8 @@
     for b in range(3):
         got0[owners[b]] = sendp[2 * b + mine]
 
+    to_odd(gates, gsend, grecv)
+
     drain(got0.at[pl.ds(0, 3)], precv)
     drain(got0.at[pl.ds(0, 2)], drecv)
 
@@ -461,20 +462,16 @@
     keys, values = keys_of(got1, group, 0, fold1, stride1, ex)
     fold_zero = jnp.zeros((fold2, LANE), F32)
     fold_lanes = lax.broadcasted_iota(jnp.int32, (fold2, LANE), 1)
-    scores = [dot_t(query, keys) for query in queries]
-    finals = []
     for i in range(2):
-        shape = (scores[i].shape[0], LANE)
-        top = jnp.broadcast_to(jnp.max(scores[i], axis=1, keepdims=True), shape)
+        scores = dot_t(queries[i], keys)
+        shape = (scores.shape[0], LANE)
+        top = jnp.broadcast_to(jnp.max(scores, axis=1, keepdims=True), shape)
         top = jnp.maximum(top, top_s[i])
-        prob = jnp.exp2(scores[i] - wide(top, scores[i].shape[1] // LANE))
+        prob = jnp.exp2(scores - wide(top, scores.shape[1] // LANE))
         total = jnp.broadcast_to(jnp.sum(prob, axis=1, keepdims=True), shape)
         decay = jnp.exp2(top_s[i] - top)
         share = 1.0 / (total_s[i] * decay + total)
-        finals.append((prob.astype(BF16), decay * share, share))
-    for i in range(2):
-        prob, old, new = finals[i]
-        mixed = o_s[i] * wide(old, 2) + dot(prob, values) * wide(new, 2)
+        mixed = o_s[i] * wide(decay * share, 2) + dot(prob.astype(BF16), values) * wide(share, 2)
         main = jnp.where(first_head, mixed[:cells, :LANE], mixed[cells:, :LANE])
         extra = mixed[cells:, LANE:]
         for s in range(half):

time: 24.5 us -> 24.4 us (level)
  no operation moved by 1% of the time
where the time goes in v7:
time: 24.4 us; the launch traced here: 24.2 us
  Pallas kernels  22.9 us (94%)
  between operations  0.66 us (3%)
  local copies, waits for them, and re-layouts  0.65 us (3%)
    pallas_call x1, Pallas kernels, per_device(): pl.pallas_call(functools.partial(block_kernel, n, rows, width, head), out...  22.9 us
    unnamed x1, local copies, waits for them, and re-layouts  0.65 us

profile of v7, /device:TPU:0, one launch (start us, length us, event | category | flops | bytes accessed | tf_op | source)
XLA Modules:
  0.0 24.2 jit_solution(7670045505807936901)
XLA Ops:
  0.7 22.9 %shard_map.109 = bf16[48,1152]{1,0:T(8,128)(2,1)S(1)} custom-call(s32[16]{0:T(128)} %counts_h.1, s32[1]{0:T(128)S(6)} %copy.14.tstep_h, s32[2,48]{1,0:T(2,128)} %pos_h.1, f32[2,1152]{1,0:T(2,128)} %constant.4.clone.pos_tab_h, f32[2,256]{1,0:T(2,128)} %constant.5.clone.time_tab_h, bf16[48,1152]{1,0:T(8,128)(2,1)} %tok_h.1, bf16[256,1152]{1,0:T(8,128)(2,1)} %tin_h.1, ...), custom_call_target="tpu_custom_call" | custom-call | tf_op jit(solution)/shard_map/pallas_call | solution.py:572
  23.6 0.6 %copy.13 = bf16[48,1152]{1,0:T(8,128)(2,1)} copy(bf16[48,1152]{1,0:T(8,128)(2,1)S(1)} %shard_map.109) | data formatting | bytes 221184
